TPU v7x, 32 devices: a whole 2x2x4 slice. The times are simulated.
32 devices in a mesh: dp: 8 (over y, x, core), tensor: 4 (over z).
Axes of the slice: x: 2, y: 2, z: 4, core: 2. Of those that a mesh axis runs over, the one named last changes fastest.
Arguments:
- tokens: bfloat16 [9216, 2048], P(('dp', 'tensor')), may hold values from -6 to 6
- segment_ids: int32 [8, 1152], P('dp'), may hold values from 0 to 2, as said below
- attn_gain: bfloat16 [1, 2048], P(None, 'dp'), may hold values from 0.5 to 1.5
- q_weight: bfloat16 [1, 2048, 2048], P(None, 'dp', 'tensor'), may hold values from -0.125 to 0.125
- key_matrix: bfloat16 [1, 2048, 1024], P(None, 'dp', 'tensor'), may hold values from -0.125 to 0.125
- value_matrix: bfloat16 [1, 2048, 1024], P(None, 'dp', 'tensor'), may hold values from -0.125 to 0.125
- o_weight: bfloat16 [1, 2048, 2048], P(None, 'dp', 'tensor'), may hold values from -0.75 to 0.75
- q_gain: bfloat16 [1, 128], P(None, 'dp'), may hold values from 0.25 to 1.75
- k_gain: bfloat16 [1, 128], P(None, 'dp'), may hold values from 0.25 to 1.75
- mlp_gain: bfloat16 [1, 2048], P(None, 'dp'), may hold values from 0.5 to 1.5
- gate_weight: bfloat16 [1, 2048, 6144], P(None, 'dp', 'tensor'), may hold values from -0.125 to 0.125
- up_weight: bfloat16 [1, 2048, 6144], P(None, 'dp', 'tensor'), may hold values from -0.125 to 0.125
- down_weight: bfloat16 [1, 2048, 6144], P(None, 'dp', 'tensor'), may hold values from -0.078125 to 0.078125
- cotangent: bfloat16 [9216, 2048], P(('dp', 'tensor')), may hold values from -6 to 6
Outputs:
- activations: bfloat16 [9216, 2048], P(('dp', 'tensor'))
- input_grad: float32 [9216, 2048], P(('dp', 'tensor'))
- attn_gain_grad: float32 [1, 2048], P(None, 'dp')
- q_weight_grad: float32 [1, 2048, 2048], P(None, 'dp', 'tensor')
- k_weight_grad: float32 [1, 2048, 1024], P(None, 'dp', 'tensor')
- v_weight_grad: float32 [1, 2048, 1024], P(None, 'dp', 'tensor')
- o_weight_grad: float32 [1, 2048, 2048], P(None, 'dp', 'tensor')
- q_gain_grad: float32 [1, 128], P(None, 'dp')
- k_gain_grad: float32 [1, 128], P(None, 'dp')
- mlp_gain_grad: float32 [1, 2048], P(None, 'dp')
- gate_weight_grad: float32 [1, 2048, 6144], P(None, 'dp', 'tensor')
- up_weight_grad: float32 [1, 2048, 6144], P(None, 'dp', 'tensor')
- down_weight_grad: float32 [1, 2048, 6144], P(None, 'dp', 'tensor')
Inputs may be any that keep to these rules, and one draw needn't show every extreme that they name: `segment_ids`: in each group the numbers never fall, each of the 3 sequences has one token or more, and one sequence of each group has exactly 1024 tokens.
All inputs are finite; a program needn't handle non-finite values.
Results may differ from a plain program's by a relative error of at most 0.02.
Values may be sent and summed in bfloat16 or wider, within the bound.
A program may use at most 192 MiB of HBM per device.

v0:
```python
import jax
import jax.numpy as jnp
from jax import lax
from jax.sharding import Mesh
from jax.sharding import PartitionSpec as P

HEAD_WIDTH = 128
DECODER_LAYERS = 1
NSEQ = 3
QBLOCK = 576
EPS = 1e-06
THETA = 1000000.0


def rms_scale(values, gain):
    return values * lax.rsqrt(jnp.mean(values * values, axis=-1, keepdims=True) + EPS) * gain


def rotate(values, cosine, sine_table):
    half_size = values.shape[-1] // 2
    turned = jnp.concatenate([-values[..., half_size:], values[..., :half_size]], axis=-1)
    return values * cosine + turned * sine_table


def swiglu(gate_raw, up_raw):
    return jax.nn.silu(gate_raw) * up_raw


def rotary_tables(sequence_labels, row_index):
    labels = jnp.arange(NSEQ, dtype=jnp.int32)
    starts = jnp.sum((sequence_labels[None, :] < labels[:, None]).astype(jnp.int32), axis=1)
    first_row = jnp.sum(
        jnp.where(sequence_labels[:, None] == labels[None, :], starts[None, :], 0), axis=1
    )
    position = (row_index - first_row).astype(jnp.float32)
    frequency = THETA ** (-(jnp.arange(HEAD_WIDTH // 2, dtype=jnp.float32) * (2.0 / HEAD_WIDTH)))
    angles = position[:, None] * frequency[None, :]
    cosine = jnp.concatenate([jnp.cos(angles), jnp.cos(angles)], axis=1)[:, None, :]
    sine_table = jnp.concatenate([jnp.sin(angles), jnp.sin(angles)], axis=1)[:, None, :]
    return (cosine, sine_table)


def contract_rows(left, right):
    return lax.dot_general(
        left, right, (((0,), (0,)), ((), ())), preferred_element_type=jnp.float32
    )


def contract_cols(left, right):
    return lax.dot_general(
        left, right, (((1,), (1,)), ((), ())), preferred_element_type=jnp.float32
    )


def block_items(queries, sequence_labels, columns):
    grouped_rows, kv_heads, repeat, head_size = queries.shape
    blocks = grouped_rows // QBLOCK
    return (
        (
            queries.reshape(blocks, QBLOCK, kv_heads, repeat, head_size),
            sequence_labels.reshape(blocks, QBLOCK),
            columns.reshape(blocks, QBLOCK),
        ),
        columns,
    )


def attend_forward(queries, key_reduced, value_reduced, sequence_labels, row_index):
    grouped_rows, kv_heads, repeat, head_size = queries.shape
    score_scale = HEAD_WIDTH ** (-0.5)
    items, columns = block_items(queries, sequence_labels, row_index)

    def one_block(block_item):
        q_block, id_block, row_block = block_item
        allowed = (id_block[:, None] == sequence_labels[None, :]) & (
            columns[None, :] <= row_block[:, None]
        )
        scores = (
            jnp.einsum("qgrd,kgd->grqk", q_block, key_reduced, preferred_element_type=jnp.float32)
            * score_scale
        )
        weights = jnp.where(allowed[None, None], jnp.exp(scores), 0.0)
        totals = jnp.sum(weights, axis=-1, keepdims=True)
        shares = (weights / totals).astype(jnp.bfloat16)
        attention_result = jnp.einsum(
            "grqk,kgd->qgrd", shares, value_reduced, preferred_element_type=jnp.float32
        )
        return (attention_result.astype(jnp.bfloat16), totals)

    attention_result, totals = lax.map(one_block, items)
    return (attention_result.reshape(grouped_rows, kv_heads * repeat * head_size), totals)


def attend_backward(
    queries, key_reduced, value_reduced, sequence_labels, row_index, totals, out_grad
):
    grouped_rows, kv_heads, repeat, head_size = queries.shape
    score_scale = HEAD_WIDTH ** (-0.5)
    items, columns = block_items(queries, sequence_labels, row_index)
    grad_blocks = out_grad.reshape(grouped_rows // QBLOCK, QBLOCK, kv_heads, repeat, head_size)

    def one_block(running, block_item):
        key_grad, value_grad = running
        q_block, id_block, row_block, total_block, grad_block = block_item
        allowed = (id_block[:, None] == sequence_labels[None, :]) & (
            columns[None, :] <= row_block[:, None]
        )
        scores = (
            jnp.einsum("qgrd,kgd->grqk", q_block, key_reduced, preferred_element_type=jnp.float32)
            * score_scale
        )
        shares = jnp.where(allowed[None, None], jnp.exp(scores), 0.0) / total_block
        low_shares = shares.astype(jnp.bfloat16)
        share_grad = jnp.einsum(
            "qgrd,kgd->grqk", grad_block, value_reduced, preferred_element_type=jnp.float32
        )
        row_inner = jnp.sum(shares * share_grad, axis=-1, keepdims=True)
        score_grad = (shares * (share_grad - row_inner)).astype(jnp.bfloat16)
        query_grad = (
            jnp.einsum(
                "grqk,kgd->qgrd", score_grad, key_reduced, preferred_element_type=jnp.float32
            )
            * score_scale
        )
        key_grad = (
            key_grad
            + jnp.einsum("grqk,qgrd->kgd", score_grad, q_block, preferred_element_type=jnp.float32)
            * score_scale
        )
        value_grad = value_grad + jnp.einsum(
            "grqk,qgrd->kgd", low_shares, grad_block, preferred_element_type=jnp.float32
        )
        return ((key_grad, value_grad), query_grad)

    zero_keys = jnp.zeros(key_reduced.shape, jnp.float32)
    (key_grad, value_grad), query_grad = lax.scan(
        one_block, (zero_keys, zero_keys), items + (totals, grad_blocks)
    )
    return (query_grad.reshape(grouped_rows, kv_heads * repeat, head_size), key_grad, value_grad)


def shift_perm(size, step):
    return [((place + step) % size, place) for place in range(size)]


def trade(values):
    return lax.ppermute(values, ("c", "h"), [(0, 0), (1, 2), (2, 1), (3, 3)])


def gather_tokens(own):
    places = lax.axis_size("l")
    parts = [own] + [lax.ppermute(own, "l", shift_perm(places, step)) for step in range(1, places)]
    half = jnp.concatenate(parts, axis=0)
    return jnp.concatenate([half, lax.ppermute(half, "c", shift_perm(2, 1))], axis=0)


def scatter_tokens(partial):
    places = lax.axis_size("l")
    half = partial.shape[0] // 2
    rows = half // places
    other = lax.ppermute(partial[half:].astype(jnp.bfloat16), "c", shift_perm(2, 1))
    total = partial[:half] + other.astype(jnp.float32)
    own = total[:rows]
    for step in range(1, places):
        sent = total[step * rows : (step + 1) * rows].astype(jnp.bfloat16)
        own = own + lax.ppermute(sent, "l", shift_perm(places, -step)).astype(jnp.float32)
    return own


def gather_weights(shard):
    core, upper = (lax.axis_index("c"), lax.axis_index("h"))
    far = lax.ppermute(shard, "h", shift_perm(2, 1))
    same = core == upper
    mine = jnp.where(same, shard, far)
    other = lax.ppermute(jnp.where(same, far, shard), "c", shift_perm(2, 1))
    rows = jnp.concatenate(
        [jnp.where(core == 0, mine, other), jnp.where(core == 0, other, mine)], axis=0
    )
    return lax.all_gather(rows, "d", axis=0, tiled=True)


def scatter_weights(partial):
    core, upper = (lax.axis_index("c"), lax.axis_index("h"))
    rows = lax.psum_scatter(partial.astype(jnp.bfloat16), "d", scatter_dimension=0, tiled=True)
    half = rows.shape[0] // 2
    first, second = (rows[:half], rows[half:])
    mine = jnp.where(core == 0, first, second)
    other = lax.ppermute(jnp.where(core == 0, second, first), "c", shift_perm(2, 1))
    same = core == upper
    far = lax.ppermute(jnp.where(same, other, mine), "h", shift_perm(2, 1))
    return jnp.where(same, mine, other).astype(jnp.float32) + far.astype(jnp.float32)


def per_device(
    tokens,
    segment_ids,
    attn_gain,
    q_weight,
    key_matrix,
    value_matrix,
    o_weight,
    q_gain,
    k_gain,
    mlp_gain,
    gate_weight,
    up_weight,
    down_weight,
    cotangent,
):
    width = attn_gain.shape[1] * lax.axis_size("d") * 2
    own_rows = tokens.shape[0]
    places = lax.axis_size("l")
    core, place = (lax.axis_index("c"), lax.axis_index("l"))
    q_cols, kv_cols, ff_cols = (q_weight.shape[2], key_matrix.shape[2], gate_weight.shape[2])
    tokens = trade(tokens)
    labels = trade(segment_ids)[0]
    attn_weights = gather_weights(
        jnp.concatenate([q_weight[0], key_matrix[0], value_matrix[0], o_weight[0]], axis=1)
    )
    mid_weights = gather_weights(jnp.concatenate([gate_weight[0], up_weight[0]], axis=1))
    down_full = gather_weights(down_weight[0])
    cotangent = trade(cotangent)
    gains = lax.all_gather(
        jnp.concatenate([attn_gain[0], mlp_gain[0], q_gain[0], k_gain[0]]), ("d", "c"), axis=0
    ).astype(jnp.float32)
    cut = attn_gain.shape[1]
    head_cut = q_gain.shape[1]
    attn_scale = gains[:, :cut].reshape(-1)
    mlp_scale = gains[:, cut : 2 * cut].reshape(-1)
    q_scale = gains[:, 2 * cut : 2 * cut + head_cut].reshape(-1)
    k_scale = gains[:, 2 * cut + head_cut :].reshape(-1)
    order = jnp.stack(
        [
            (core + core_step) % 2 * places + (place + step) % places
            for core_step in range(2)
            for step in range(places)
        ]
    )
    row_index = (
        order[:, None] * own_rows + jnp.arange(own_rows, dtype=jnp.int32)[None, :]
    ).reshape(-1)
    labels = labels.reshape(2 * places, own_rows)[order].reshape(-1)
    cosine, sine_table = rotary_tables(labels, row_index)
    stream = tokens.astype(jnp.float32)
    normed = gather_tokens(rms_scale(stream, attn_scale).astype(jnp.bfloat16))
    rows = normed.shape[0]
    head_count, kv_heads = (q_cols // HEAD_WIDTH, kv_cols // HEAD_WIDTH)
    q_full = attn_weights[:, :q_cols]
    k_full = attn_weights[:, q_cols : q_cols + kv_cols]
    v_full = attn_weights[:, q_cols + kv_cols : q_cols + 2 * kv_cols]
    o_full = attn_weights[:, q_cols + 2 * kv_cols :]
    queries = jnp.dot(normed, q_full, preferred_element_type=jnp.float32).reshape(
        rows, head_count, HEAD_WIDTH
    )
    keys = jnp.dot(normed, k_full, preferred_element_type=jnp.float32).reshape(
        rows, kv_heads, HEAD_WIDTH
    )
    value_reduced = (
        jnp.dot(normed, v_full, preferred_element_type=jnp.float32)
        .reshape(rows, kv_heads, HEAD_WIDTH)
        .astype(jnp.bfloat16)
    )
    query_reduced = rotate(rms_scale(queries, q_scale), cosine, sine_table).astype(jnp.bfloat16)
    key_reduced = rotate(rms_scale(keys, k_scale), cosine, sine_table).astype(jnp.bfloat16)
    query_reduced = query_reduced.reshape(rows, kv_heads, head_count // kv_heads, HEAD_WIDTH)
    attended, totals = attend_forward(query_reduced, key_reduced, value_reduced, labels, row_index)
    middle = stream + scatter_tokens(contract_cols(attended, o_full))
    normed_mid = gather_tokens(rms_scale(middle, mlp_scale).astype(jnp.bfloat16))
    gate_full, up_full = (mid_weights[:, :ff_cols], mid_weights[:, ff_cols:])
    gate_raw = jnp.dot(normed_mid, gate_full, preferred_element_type=jnp.float32)
    up_raw = jnp.dot(normed_mid, up_full, preferred_element_type=jnp.float32)
    hidden = swiglu(gate_raw, up_raw).astype(jnp.bfloat16)
    branch = scatter_tokens(contract_cols(hidden, down_full))
    activations = trade((middle + branch).astype(jnp.bfloat16))
    grad_rows = gather_tokens(cotangent)
    gradient = cotangent.astype(jnp.float32)
    down_grad = scatter_weights(contract_rows(grad_rows, hidden))
    hidden_grad = jnp.dot(grad_rows, down_full, preferred_element_type=jnp.float32)
    _, pull_back = jax.vjp(swiglu, gate_raw, up_raw)
    gate_grad, up_grad = pull_back(hidden_grad)
    gate_low = gate_grad.astype(jnp.bfloat16)
    up_low = up_grad.astype(jnp.bfloat16)
    mid_grad = scatter_weights(
        jnp.concatenate(
            [
                contract_rows(normed_mid, gate_low).astype(jnp.bfloat16),
                contract_rows(normed_mid, up_low).astype(jnp.bfloat16),
            ],
            axis=1,
        )
    )
    normed_grad = scatter_tokens(
        contract_cols(gate_low, gate_full) + contract_cols(up_low, up_full)
    )
    _, pull_norm = jax.vjp(rms_scale, middle, mlp_scale)
    middle_grad, mlp_gain_grad = pull_norm(normed_grad)
    gradient = gradient + middle_grad
    grad_rows = gather_tokens(gradient.astype(jnp.bfloat16))
    out_grad = jnp.dot(grad_rows, o_full, preferred_element_type=jnp.float32).astype(jnp.bfloat16)
    o_wgrad = contract_rows(grad_rows, attended)
    query_grad, key_grad, value_grad = attend_backward(
        query_reduced,
        key_reduced,
        value_reduced,
        labels,
        row_index,
        totals,
        out_grad.reshape(query_reduced.shape),
    )

    def query_path(raw_values, scales):
        return rotate(rms_scale(raw_values, scales), cosine, sine_table)

    _, pull_query = jax.vjp(query_path, queries, q_scale)
    query_raw_grad, q_gain_grad = pull_query(query_grad)
    _, pull_key = jax.vjp(query_path, keys, k_scale)
    key_raw_grad, k_gain_grad = pull_key(key_grad)
    query_back = query_raw_grad.reshape(rows, -1).astype(jnp.bfloat16)
    key_back = key_raw_grad.reshape(rows, -1).astype(jnp.bfloat16)
    value_back = value_grad.reshape(rows, -1).astype(jnp.bfloat16)
    attn_grad = scatter_weights(
        jnp.concatenate(
            [
                contract_rows(normed, query_back).astype(jnp.bfloat16),
                contract_rows(normed, key_back).astype(jnp.bfloat16),
                contract_rows(normed, value_back).astype(jnp.bfloat16),
                o_wgrad.astype(jnp.bfloat16),
            ],
            axis=1,
        )
    )
    normed_grad = scatter_tokens(
        contract_cols(query_back, q_full)
        + contract_cols(key_back, k_full)
        + contract_cols(value_back, v_full)
    )
    _, pull_norm = jax.vjp(rms_scale, stream, attn_scale)
    stream_grad, attn_gain_grad = pull_norm(normed_grad)
    gradient = gradient + stream_grad
    moved = trade(gradient.astype(jnp.bfloat16))
    gradient = jnp.where(core == lax.axis_index("h"), gradient, moved.astype(jnp.float32))
    sums = lax.psum(
        jnp.concatenate([attn_gain_grad, mlp_gain_grad, q_gain_grad, k_gain_grad]),
        ("d", "c", "h", "l"),
    )
    row = lax.axis_index("d") * 2 + core

    def owned(start, whole, part):
        return lax.dynamic_slice(sums[start : start + whole], (row * part,), (part,))[None]

    return (
        activations,
        gradient,
        owned(0, width, cut),
        attn_grad[None, :, :q_cols],
        attn_grad[None, :, q_cols : q_cols + kv_cols],
        attn_grad[None, :, q_cols + kv_cols : q_cols + 2 * kv_cols],
        attn_grad[None, :, q_cols + 2 * kv_cols :],
        owned(2 * width, HEAD_WIDTH, head_cut),
        owned(2 * width + HEAD_WIDTH, HEAD_WIDTH, head_cut),
        owned(width, width, cut),
        mid_grad[None, :, :ff_cols],
        mid_grad[None, :, ff_cols:],
        down_grad[None],
    )


def solution(mesh):
    dp, tensor = (mesh.shape["dp"], mesh.shape["tensor"])
    cut = Mesh(mesh.devices.reshape(dp // 2, 2, 2, tensor // 2), ("d", "c", "h", "l"))
    rows, cols = (("d", "c"), ("h", "l"))
    tokens, labels = (P(rows + cols, None), P(rows, None))
    gain, weight = (P(None, rows), P(None, rows, cols))
    return jax.shard_map(
        per_device,
        mesh=cut,
        in_specs=(
            tokens,
            labels,
            gain,
            weight,
            weight,
            weight,
            weight,
            gain,
            gain,
            gain,
            weight,
            weight,
            weight,
            tokens,
        ),
        out_specs=(
            tokens,
            tokens,
            gain,
            weight,
            weight,
            weight,
            weight,
            gain,
            gain,
            gain,
            weight,
            weight,
            weight,
        ),
        check_vma=False,
    )
```

profile of v0, /device:TPU:0, one launch (start us, length us, event | category | flops | bytes accessed | tf_op | source)
XLA Modules:
  0.0 1063.8 jit_solution(16250169278718028177)
XLA Ops:
  11.5 4.1 collective-permute-start.4
  15.6 34.4 %collective-permute-done.4 = bf16[256,1536]{0,1:T(8,128)(2,1)S(1)} collective-permute-done((bf16[256,1536]{0,1:T(8,128)(2,1)S(1)}, bf16[256,1536]{0,1:T(8,128)(2,1)S(1)}, u32[]{:S(2)}, u32[]{:S(2)}) %collective-permute-start.4) | collective-permute-done | bytes 786464 | tf_op jit(solution)/shard_map/ppermute | solution.py:172
  59.5 3.3 collective-permute-start.10
  64.4 25.7 %all-reduce.4 = bf16[4352]{0:T(1024)(128)(2,1)S(1)} all-reduce(bf16[4352]{0:T(1024)(128)(2,1)S(1)} %dynamic-update-slice), channel_id=2, replica_groups=mesh['d'=4,'c'=2,'h'=2,'l'=2] {'d','c'}, use_global_device_ids=true, to_apply=%add.4 | all-reduce | flops 4352 | bytes 17408
  102.3 51.4 %collective-permute-done.10 = bf16[256,3072]{0,1:T(8,128)(2,1)} collective-permute-done((bf16[256,3072]{0,1:T(8,128)(2,1)}, bf16[256,3072]{0,1:T(8,128)(2,1)}, u32[]{:S(2)}, u32[]{:S(2)}) %collective-permute-start.10) | collective-permute-done | bytes 1572896 | tf_op jit(solution)/shard_map/ppermute | solution.py:172
  155.6 9.9 collective-permute-done.2
  167.3 6.5 collective-permute-start.3
  180.8 3.5 multiply_reduce_fusion.8
  186.1 7.4 multiply_reduce_fusion.5
  200.7 3.8 copy.194
  204.5 5.0 copy.192
  210.8 7.0 fusion.70
  219.4 4.4 convolution_convert_fusion.8
  225.2 25.8 %while.28 = (s32[]{:T(128)}, bf16[2,576,2,2,128]{4,3,2,1,0:T(2,128)(2,1)S(1)}, f32[2,2,2,576,1]{3,2,1,4,0:T(2,128)}, s32[2,576]{1,0:T(2,128)}, s32[4,288]{1,0:T(...) while((s32[]{:T(128)}, ...), condition=%wide.region_7.8_spmd.clone, body=%wide.region_5.7_spmd.clone.sunk | while | flops 1379818368 | bytes 26884800 | solution.py:90
  230.6 3.1 bitcast_reduce_fusion.2
  233.7 3.1 fusion.140
  243.5 3.1 bitcast_reduce_fusion.2
  246.6 3.1 fusion.140
  252.1 15.6 %reshape.558 = bf16[1152,512]{1,0:T(8,128)(2,1)S(1)} reshape(bf16[2,576,2,2,128]{4,3,2,1,0:T(2,128)(2,1)} %copy-done.46) | data formatting | bytes 2359296 | tf_op jit(solution)/shard_map/reshape | solution.py:91
  267.7 4.6 fusion.72
  279.7 36.7 %collective-permute-done.12 = bf16[256,1536]{0,1:T(8,128)(2,1)S(1)} collective-permute-done((bf16[256,1536]{0,1:T(8,128)(2,1)S(1)}, bf16[256,1536]{0,1:T(8,128)(2,1)S(1)}, u32[]{:S(2)}, u32[]{:S(2)}) %collective-permute-start.12) | collective-permute-done | bytes 786464 | tf_op jit(solution)/shard_map/ppermute | solution.py:172
  316.6 10.4 collective-permute-start.17
  335.1 37.7 %collective-permute-done.7 = bf16[288,2048]{1,0:T(8,128)(2,1)} collective-permute-done((bf16[288,2048]{1,0:T(8,128)(2,1)}, bf16[288,2048]{1,0:T(8,128)(2,1)}, u32[]{:S(2)}, u32[]{:S(2)}) %collective-permute-start.7) | collective-permute-done | bytes 1179680 | tf_op jit(solution)/shard_map/ppermute | solution.py:166
  375.8 22.1 %collective-permute-done.18 = bf16[288,2048]{1,0:T(8,128)(2,1)S(1)} collective-permute-done((bf16[288,2048]{1,0:T(8,128)(2,1)}, bf16[288,2048]{1,0:T(8,128)(2,1)S(1)}, u32[]{:S(2)}, u32[]{:S(2)}) %collective-permute-start.18) | collective-permute-done | bytes 1179680 | tf_op jit(solution)/shard_map/ppermute | solution.py:152
  399.5 15.3 %collective-permute-done.8 = bf16[288,2048]{1,0:T(8,128)(2,1)S(1)} collective-permute-done((bf16[288,2048]{1,0:T(8,128)(2,1)S(1)}, bf16[288,2048]{1,0:T(8,128)(2,1)S(1)}, u32[]{:S(2)}, u32[]{:S(2)}) %collective-permute-start.8) | collective-permute-done | bytes 1179680 | tf_op jit(solution)/shard_map/ppermute | solution.py:152
  419.8 12.7 %fusion.52 = f32[1152,1536]{1,0:T(8,128)} fusion(bf16[2048,3072]{0,1:T(8,128)(2,1)} %all-gather.7.cloned.1.call-done, bf16[576,2048]{1,0:T(8,128)(2,1)} %collective-permute-done.9, bf16[288,2048]{1,0:T(8,128)(2,1)} %copy-done.51, bf16[288,2048]{1,0:T(8,128)(2,1)S(1)} %multiply_convert_fusion.2), kind=kOutput, calls=%fused_computation.75 | convolution fusion | flops 7261913088 | bytes 18087936 | tf_op jit(solution)/shard_map/dot_general | solution.py:271
  432.6 11.0 %fusion.56 = f32[1152,1536]{1,0:T(8,128)} fusion(bf16[2048,3072]{0,1:T(8,128)(2,1)S(1)} %copy-done.94, bf16[576,2048]{1,0:T(8,128)(2,1)} %collective-permute-done.9, bf16[288,2048]{1,0:T(8,128)(2,1)S(1)} %copy-done.52, bf16[288,2048]{1,0:T(8,128)(2,1)S(1)} %multiply_convert_fusion.2), kind=kOutput, calls=%fused_computation.79 | convolution fusion | flops 7261913088 | bytes 18087936 | tf_op jit(solution)/shard_map/dot_general | solution.py:270
  443.5 18.9 %multiply_convert_fusion = (bf16[1152,1536]{1,0:T(8,128)(2,1)}, bf16[1152,1536]{1,0:T(8,128)(2,1)}, bf16[1152,1536]{1,0:T(8,128)(2,1)}) fusion(f32[1152,1536]{1,0:T(8,128)} %fusion.56, f32[1152,1536]{1,0:T(8,128)} %fusion.52, bf16[1152,2048]{1,0:T(8,128)(2,1)} %copy-done.64, bf16[2048,1536]{0,1:T(8,128)(2,1)} %all-gather.9.cloned.1.call-done), kind=kOutput, calls=%fused_computation.69 | convolution fusion | flops 7276068864 | bytes 35782656 | tf_op jit(solution)/shard_map/dot_general | solution.py:278
  462.5 11.2 %fusion.54 = f32[1152,2048]{1,0:T(8,128)S(1)} fusion(bf16[1152,1536]{1,0:T(8,128)(2,1)} %get-tuple-element.461, bf16[2048,3072]{0,1:T(8,128)(2,1)} %all-gather.7.cloned.1.call-done), kind=kOutput, calls=%fused_computation.77 | convolution fusion | flops 7247757312 | bytes 19267584 | tf_op jit(solution)/shard_map/dot_general | solution.py:50
  473.7 10.9 %convolution_add_fusion.2 = f32[1152,2048]{1,0:T(8,128)S(1)} fusion(f32[1152,2048]{1,0:T(8,128)S(1)} %fusion.54, bf16[1152,1536]{1,0:T(8,128)(2,1)} %get-tuple-element.460, bf16[2048,3072]{0,1:T(8,128)(2,1)} %all-gather.7.cloned.1.call-done), kind=kOutput, calls=%fused_computation.62 | convolution fusion | flops 7250116608 | bytes 28704768 | tf_op jit(solution)/shard_map/dot_general | solution.py:50
  485.2 3.8 copy-done.29
  489.3 10.0 fusion.102
  499.9 3.1 slice_add_fusion.1
  506.5 25.5 %collective-permute-done.21 = bf16[288,2048]{1,0:T(8,128)(2,1)S(1)} collective-permute-done((bf16[288,2048]{1,0:T(8,128)(2,1)S(1)}, bf16[288,2048]{1,0:T(8,128)(2,1)S(1)}, u32[]{:S(2)}, u32[]{:S(2)}) %collective-permute-start.21) | collective-permute-done | bytes 1179680 | tf_op jit(solution)/shard_map/ppermute | solution.py:166
  533.4 23.3 %collective-permute-done.15 = bf16[288,2048]{1,0:T(8,128)(2,1)S(1)} collective-permute-done((bf16[288,2048]{1,0:T(8,128)(2,1)S(1)}, bf16[288,2048]{1,0:T(8,128)(2,1)S(1)}, u32[]{:S(2)}, u32[]{:S(2)}) %collective-permute-start.15) | collective-permute-done | bytes 1179680 | tf_op jit(solution)/shard_map/ppermute | solution.py:166
  556.7 4.4 fusion.95
  561.4 27.1 %collective-permute-done.22 = bf16[288,2048]{1,0:T(8,128)(2,1)S(1)} collective-permute-done((bf16[288,2048]{1,0:T(8,128)(2,1)S(1)}, bf16[288,2048]{1,0:T(8,128)(2,1)S(1)}, u32[]{:S(2)}, u32[]{:S(2)}) %collective-permute-start.22) | collective-permute-done | bytes 1179680 | tf_op jit(solution)/shard_map/ppermute | solution.py:152
  591.2 13.1 %convolution_convert_fusion = bf16[2048,1536]{0,1:T(8,128)(2,1)} fusion(bf16[1152,2048]{1,0:T(8,128)(2,1)} %copy-done.64, bf16[1152,1536]{1,0:T(8,128)(2,1)} %get-tuple-element.462), kind=kOutput, calls=%fused_computation.63 | convolution fusion | flops 7250903040 | bytes 14548992 | tf_op jit(solution)/shard_map/dot_general | solution.py:44
  604.4 6.3 convolution_convert_fusion.5
  610.7 3.8 reshape_reshape.5
  614.5 55.6 %while.29 = (s32[]{:T(128)}, f32[1152,2,128]{0,2,1:T(8,128)S(1)}, f32[1152,2,128]{0,2,1:T(8,128)S(1)}, f32[2,576,2,2,128]{4,1,0,3,2:T(8,128)}, bf16[2,576,2,2,12...) while((s32[]{:T(128)}, f32[1152,2,128]{0,2,1:T(8,128)S(1)}, ...), condition=%wide.region_12.13_spmd.clone, body=%wide.region_10.12_spmd.clone.sunk | while | flops 3425033216 | bytes 203141424 | solution.py:136
  622.2 4.0 fusion.148
  635.1 4.2 fusion.150
  649.7 4.0 fusion.148
  662.7 4.4 fusion.150
  670.1 3.3 copy.175
  681.6 3.2 convolution_convert_fusion.7
  684.8 3.4 convolution_convert_fusion.6
  688.2 4.7 convolution_convert_fusion.4
  693.4 5.0 convolution_convert_fusion.3
  698.5 12.4 %pad_maximum_fusion.1 = bf16[2048,1536]{0,1:T(8,128)(2,1)} fusion(bf16[2048,512]{0,1:T(8,128)(2,1)S(1)} %convolution_convert_fusion.4, bf16[2048,256]{0,1:T(8,128)(2,1)S(1)} %convolution_convert_fusion.6, bf16[2048,256]{0,1:T(8,128)(2,1)S(1)} %convolution_convert_fusion.7, bf16[2048,512]{0,1:T(8,128)(2,1)S(1)} %convolution_convert_fusion.3), kind=kLoop, calls=%fused_computation.73 | loop fusion | flops 25165824 | bytes 12582912 | tf_op jit(solution)/shard_map/concatenate | solution.py:322
  712.5 11.2 %convolution_convert_fusion.2 = bf16[2048,1536]{0,1:T(8,128)(2,1)S(1)} fusion(bf16[1152,1536]{1,0:T(8,128)(2,1)} %get-tuple-element.461, bf16[576,2048]{1,0:T(8,128)(2,1)} %collective-permute-done.9, bf16[288,2048]{1,0:T(8,128)(2,1)S(1)} %copy-done.53, bf16[288,2048]{1,0:T(8,128)(2,1)S(1)} %copy-done.31), kind=kOutput, calls=%fused_computation.65 | convolution fusion | flops 7265058816 | bytes 14548992 | tf_op jit(solution)/shard_map/dot_general | solution.py:44
  723.7 10.2 convolution_convert_fusion.1
  733.9 15.3 %pad_maximum_fusion = bf16[2048,3072]{0,1:T(8,128)(2,1)} fusion(bf16[2048,1536]{0,1:T(8,128)(2,1)S(1)} %convolution_convert_fusion.1, bf16[2048,1536]{0,1:T(8,128)(2,1)S(1)} %convolution_convert_fusion.2), kind=kLoop, calls=%fused_computation.58 | loop fusion | flops 25165824 | bytes 25165824 | tf_op jit(solution)/shard_map/concatenate | solution.py:284
  750.6 4.2 fusion.74
  770.4 39.9 %collective-permute-done.25 = bf16[288,2048]{1,0:T(8,128)(2,1)S(1)} collective-permute-done((bf16[288,2048]{1,0:T(8,128)(2,1)}, bf16[288,2048]{1,0:T(8,128)(2,1)S(1)}, u32[]{:S(2)}, u32[]{:S(2)}) %collective-permute-start.25) | collective-permute-done | bytes 1179680 | tf_op jit(solution)/shard_map/ppermute | solution.py:166
  810.4 3.6 fusion.61
  814.0 39.3 %psum.7 = f32[4352]{0:T(1024)S(1)} all-reduce(f32[4352]{0:T(1024)S(1)} %pad_maximum_fusion.20), channel_id=1, replica_groups=mesh['d'=4,'c'=2,'h'=2,'l'=2] {'d','c','h','l'}, use_global_device_ids=true, to_apply=%region_20.21 | all-reduce | flops 4352 | bytes 34816 | tf_op jit(solution)/shard_map/psum | solution.py:342
  855.3 4.6 fusion.93
  859.8 10.6 collective-permute-start.26
  877.6 27.4 %reduce-scatter.6.cloned.1.call-done = bf16[512,3072]{0,1:T(8,128)(2,1)} async-done(((bf16[2048,3072]{0,1:T(8,128)(2,1)}), bf16[512,3072]{0,1:T(8,128)(2,1)}) %reduce-scatter.6.cloned.1.call-update) | async-done | bytes 3145744 | tf_op jit(solution)/shard_map/reduce_scatter | solution.py:184
  920.6 79.5 %collective-permute-done.32 = bf16[256,1536]{0,1:T(8,128)(2,1)S(1)} collective-permute-done((bf16[256,1536]{0,1:T(8,128)(2,1)S(1)}, bf16[256,1536]{0,1:T(8,128)(2,1)S(1)}, u32[]{:S(2)}, u32[]{:S(2)}) %collective-permute-start.32) | collective-permute-done | bytes 786464 | tf_op jit(solution)/shard_map/ppermute | solution.py:190
  1004.6 12.4 %collective-permute-done.28 = bf16[256,1536]{0,1:T(8,128)(2,1)} collective-permute-done((bf16[256,1536]{0,1:T(8,128)(2,1)}, bf16[256,1536]{0,1:T(8,128)(2,1)}, u32[]{:S(2)}, u32[]{:S(2)}) %collective-permute-start.28) | collective-permute-done | bytes 786464 | tf_op jit(solution)/shard_map/ppermute | solution.py:190
  1029.6 20.6 %collective-permute-done.30 = bf16[256,3072]{0,1:T(8,128)(2,1)} collective-permute-done((bf16[256,3072]{0,1:T(8,128)(2,1)}, bf16[256,3072]{0,1:T(8,128)(2,1)}, u32[]{:S(2)}, u32[]{:S(2)}) %collective-permute-start.30) | collective-permute-done | bytes 1572896 | tf_op jit(solution)/shard_map/ppermute | solution.py:190
  (458 shorter events, 212.8 us)
Async XLA Ops:
  7.2 172.5 %all-gather.5.cloned.1.call-start = ((), (), s32[]{:S(2)}) async-start(), calls=%async_computation.3 | async-start | bytes 7864320 | tf_op jit(solution)/shard_map/all_gather | solution.py:179
  11.5 38.5 %collective-permute-start.4 = (bf16[256,1536]{0,1:T(8,128)(2,1)S(1)}, bf16[256,1536]{0,1:T(8,128)(2,1)S(1)}, u32[]{:S(2)}, u32[]{:S(2)}) collective-permute-start(bf16[256,1536]{0,1:T(8,128)(2,1)S(1)} %pad_maximum_fusion.15), channel_id=1, source_target_pairs={{2,0},{0,2},{3,1},{1,3},{6,4},{4,6},{7,5},{5,7},{10,8},{8,10},{11,... | collective-permute-start | bytes 2359304 | tf_op jit(solution)/shard_map/ppermute | solution.py:172
  50.2 2.4 collective-permute-start.5
  54.2 365.6 %all-gather.7.cloned.1.call-start = ((), (), s32[]{:S(2)}) async-start(), calls=%async_computation.4 | async-start | bytes 15728640 | tf_op jit(solution)/shard_map/all_gather | solution.py:179
  54.3 42.5 %collective-permute-start = (bf16[288,2048]{1,0:T(8,128)(2,1)}, bf16[288,2048]{1,0:T(8,128)(2,1)S(1)}, u32[]{:S(2)}, u32[]{:S(2)}) collective-permute-start(bf16[288,2048]{1,0:T(8,128)(2,1)} %param.18), channel_id=1, source_target_pairs={{0,0},{2,4},{4,2},{6,6},{1,1},{3,5},{5,3},{7,7},{8,8},{10,12},{12,... | collective-permute-start | bytes 3538952 | tf_op jit(solution)/shard_map/ppermute | solution.py:147
  56.3 38.7 %collective-permute-start.1 = (s32[1,1152]{1,0:T(1,128)}, s32[1,1152]{1,0:T(1,128)S(1)}, u32[]{:S(2)}, u32[]{:S(2)}) collective-permute-start(s32[1,1152]{1,0:T(1,128)} %param.19), channel_id=1, source_target_pairs={{0,0},{2,4},{4,2},{6,6},{1,1},{3,5},{5,3},{7,7},{8,8},{10,12},{12,... | collective-permute-start | bytes 13832 | tf_op jit(solution)/shard_map/ppermute | solution.py:147
  59.5 94.2 %collective-permute-start.10 = (bf16[256,3072]{0,1:T(8,128)(2,1)}, bf16[256,3072]{0,1:T(8,128)(2,1)}, u32[]{:S(2)}, u32[]{:S(2)}) collective-permute-start(bf16[256,3072]{0,1:T(8,128)(2,1)} %pad_maximum_fusion.13), channel_id=1, source_target_pairs={{2,0},{0,2},{3,1},{1,3},{6,4},{4,6},{7,5},{5,7},{10,8},{8,10},{11,... | collective-permute-start | bytes 4718600 | tf_op jit(solution)/shard_map/ppermute | solution.py:172
  97.1 58.4 %copy-start.82 = (f32[288]{0:T(512)}, f32[288]{0:T(512)S(1)}, u32[]{:S(2)}) copy-start(f32[288]{0:T(512)S(1)} %fusion.65) | copy-start | bytes 3460
  97.1 58.4 %copy-start.80 = (f32[288]{0:T(512)}, f32[288]{0:T(512)S(1)}, u32[]{:S(2)}) copy-start(f32[288]{0:T(512)S(1)} %fusion.88) | copy-start | bytes 3460
  97.4 68.1 %copy-start.32 = (bf16[288,2048]{1,0:T(8,128)(2,1)}, bf16[288,2048]{1,0:T(8,128)(2,1)S(1)}, u32[]{:S(2)}) copy-start(bf16[288,2048]{1,0:T(8,128)(2,1)S(1)} %fusion.60) | copy-start | bytes 3538948
  97.4 68.0 %collective-permute-start.2 = (bf16[288,2048]{1,0:T(8,128)(2,1)S(1)}, bf16[288,2048]{1,0:T(8,128)(2,1)S(1)}, u32[]{:S(2)}, u32[]{:S(2)}) collective-permute-start(bf16[288,2048]{1,0:T(8,128)(2,1)S(1)} %fusion.60), channel_id=1, source_target_pairs={{1,0},{0,1},{3,2},{2,3},{5,4},{4,5},{7,6},{6,7},{9,8},{8,9},{11,10... | collective-permute-start | bytes 3538952 | tf_op jit(solution)/shard_map/ppermute | solution.py:152
  155.5 20.9 %collective-permute-start.11 = (bf16[256,3072]{0,1:T(8,128)(2,1)S(1)}, bf16[256,3072]{0,1:T(8,128)(2,1)S(1)}, u32[]{:S(2)}, u32[]{:S(2)}) collective-permute-start(bf16[256,3072]{0,1:T(8,128)(2,1)S(1)} %broadcast_select_fusion.1), channel_id=1, source_target_pairs={{4,0},{0,4},{5,1},{1,5},{6,2},{2,6},{7,3},{3,7},{12,8},{8,12},{13,... | collective-permute-start | bytes 4718600 | tf_op jit(solution)/shard_map/ppermute | solution.py:175
  167.3 12.3 %collective-permute-start.3 = (bf16[576,2048]{1,0:T(8,128)(2,1)}, bf16[576,2048]{1,0:T(8,128)(2,1)}, u32[]{:S(2)}, u32[]{:S(2)}) collective-permute-start(bf16[576,2048]{1,0:T(8,128)(2,1)} %pad_maximum_fusion.6), channel_id=1, source_target_pairs={{4,0},{0,4},{5,1},{1,5},{6,2},{2,6},{7,3},{3,7},{12,8},{8,12},{13,... | collective-permute-start | bytes 7077896 | tf_op jit(solution)/shard_map/ppermute | solution.py:154
  176.3 9.0 copy-start.22
  176.4 9.0 copy-start.24
  179.2 264.3 %all-gather.9.cloned.1.call-start = ((), (), s32[]{:S(2)}) async-start(), calls=%async_computation.5 | async-start | bytes 7864320 | tf_op jit(solution)/shard_map/all_gather | solution.py:179
  252.0 20.3 %copy-start.12 = (bf16[1152,2,128]{2,0,1:T(8,128)(2,1)}, bf16[1152,2,128]{2,0,1:T(8,128)(2,1)S(1)}, u32[]{:S(2)}) copy-start(bf16[1152,2,128]{2,0,1:T(8,128)(2,1)S(1)} %get-tuple-element.774) | copy-start | bytes 1769476
  252.0 20.3 %copy-start.14 = (bf16[1152,2,128]{2,0,1:T(8,128)(2,1)}, bf16[1152,2,128]{2,0,1:T(8,128)(2,1)S(1)}, u32[]{:S(2)}) copy-start(bf16[1152,2,128]{2,0,1:T(8,128)(2,1)S(1)} %get-tuple-element.775) | copy-start | bytes 1769476
  252.0 20.3 %copy-start.16 = (bf16[2,576,2,2,128]{4,1,3,2,0:T(8,128)(2,1)}, bf16[2,576,2,2,128]{4,1,3,2,0:T(8,128)(2,1)S(1)}, u32[]{:S(2)}) copy-start(bf16[2,576,2,2,128]{4,1,3,2,0:T(8,128)(2,1)S(1)} %get-tuple-element.776) | copy-start | bytes 3538948
  252.0 20.3 %copy-start.58 = (s32[4,288]{1,0:T(4,128)}, s32[4,288]{1,0:T(4,128)S(1)}, u32[]{:S(2)}) copy-start(s32[4,288]{1,0:T(4,128)S(1)} %get-tuple-element.818) | copy-start | bytes 13828
  252.0 20.4 %copy-start.69 = (s32[2,576]{1,0:T(2,128)}, s32[2,576]{1,0:T(2,128)S(1)}, u32[]{:S(2)}) copy-start(s32[2,576]{1,0:T(2,128)S(1)} %get-tuple-element.827) | copy-start | bytes 13828
  276.7 50.3 %collective-permute-start.6 = (bf16[576,2048]{1,0:T(8,128)(2,1)}, bf16[576,2048]{1,0:T(8,128)(2,1)S(1)}, u32[]{:S(2)}, u32[]{:S(2)}) collective-permute-start(bf16[576,2048]{1,0:T(8,128)(2,1)} %slice.347), channel_id=1, source_target_pairs={{4,0},{0,4},{5,1},{1,5},{6,2},{2,6},{7,3},{3,7},{12,8},{8,12},{13,... | collective-permute-start | bytes 7077896 | tf_op jit(solution)/shard_map/ppermute | solution.py:161
  279.7 36.7 %collective-permute-start.12 = (bf16[256,1536]{0,1:T(8,128)(2,1)S(1)}, bf16[256,1536]{0,1:T(8,128)(2,1)S(1)}, u32[]{:S(2)}, u32[]{:S(2)}) collective-permute-start(bf16[256,1536]{0,1:T(8,128)(2,1)S(1)} %bitcast.247), channel_id=1, source_target_pairs={{2,0},{0,2},{3,1},{1,3},{6,4},{4,6},{7,5},{5,7},{10,8},{8,10},{11,... | collective-permute-start | bytes 2359304 | tf_op jit(solution)/shard_map/ppermute | solution.py:172
  316.5 14.9 %collective-permute-start.13 = (bf16[256,1536]{0,1:T(8,128)(2,1)S(1)}, bf16[256,1536]{0,1:T(8,128)(2,1)S(1)}, u32[]{:S(2)}, u32[]{:S(2)}) collective-permute-start(bf16[256,1536]{0,1:T(8,128)(2,1)S(1)} %broadcast_select_fusion.9), channel_id=1, source_target_pairs={{4,0},{0,4},{5,1},{1,5},{6,2},{2,6},{7,3},{3,7},{12,8},{8,12},{13,... | collective-permute-start | bytes 2359304 | tf_op jit(solution)/shard_map/ppermute | solution.py:175
  316.6 17.3 %collective-permute-start.17 = (bf16[288,2048]{1,0:T(8,128)(2,1)}, bf16[288,2048]{1,0:T(8,128)(2,1)}, u32[]{:S(2)}, u32[]{:S(2)}) collective-permute-start(bf16[288,2048]{1,0:T(8,128)(2,1)} %param.31), channel_id=1, source_target_pairs={{0,0},{2,4},{4,2},{6,6},{1,1},{3,5},{5,3},{7,7},{8,8},{10,12},{12,... | collective-permute-start | bytes 3538952 | tf_op jit(solution)/shard_map/ppermute | solution.py:147
  331.4 41.4 %collective-permute-start.7 = (bf16[288,2048]{1,0:T(8,128)(2,1)}, bf16[288,2048]{1,0:T(8,128)(2,1)}, u32[]{:S(2)}, u32[]{:S(2)}) collective-permute-start(bf16[288,2048]{1,0:T(8,128)(2,1)} %slice.351), channel_id=1, source_target_pairs={{1,0},{0,1},{3,2},{2,3},{5,4},{4,5},{7,6},{6,7},{9,8},{8,9},{11,10... | collective-permute-start | bytes 3538952 | tf_op jit(solution)/shard_map/ppermute | solution.py:166
  332.5 40.3 %copy-start.8 = (bf16[288,2048]{1,0:T(8,128)(2,1)S(1)}, bf16[288,2048]{1,0:T(8,128)(2,1)}, u32[]{:S(2)}) copy-start(bf16[288,2048]{1,0:T(8,128)(2,1)} %copy-done.7) | copy-start | bytes 3538948
  333.8 538.5 %reduce-scatter.8.cloned.1.call-start = ((), (), s32[]{:S(2)}) async-start(), calls=%async_computation.8 | async-start | bytes 7864320 | tf_op jit(solution)/shard_map/reduce_scatter | solution.py:184
  333.9 64.0 %collective-permute-start.18 = (bf16[288,2048]{1,0:T(8,128)(2,1)}, bf16[288,2048]{1,0:T(8,128)(2,1)S(1)}, u32[]{:S(2)}, u32[]{:S(2)}) collective-permute-start(bf16[288,2048]{1,0:T(8,128)(2,1)} %collective-permute-done.17), channel_id=1, source_target_pairs={{1,0},{0,1},{3,2},{2,3},{5,4},{4,5},{7,6},{6,7},{9,8},{8,9},{11,10... | collective-permute-start | bytes 3538952 | tf_op jit(solution)/shard_map/ppermute | solution.py:152
  375.7 56.8 %copy-start.30 = (bf16[288,2048]{1,0:T(8,128)(2,1)}, bf16[288,2048]{1,0:T(8,128)(2,1)S(1)}, u32[]{:S(2)}) copy-start(bf16[288,2048]{1,0:T(8,128)(2,1)S(1)} %multiply_convert_fusion.2) | copy-start | bytes 3538948
  375.8 39.0 %collective-permute-start.8 = (bf16[288,2048]{1,0:T(8,128)(2,1)S(1)}, bf16[288,2048]{1,0:T(8,128)(2,1)S(1)}, u32[]{:S(2)}, u32[]{:S(2)}) collective-permute-start(bf16[288,2048]{1,0:T(8,128)(2,1)S(1)} %multiply_convert_fusion.2), channel_id=1, source_target_pairs={{1,0},{0,1},{3,2},{2,3},{5,4},{4,5},{7,6},{6,7},{9,8},{8,9},{11,10... | collective-permute-start | bytes 3538952 | tf_op jit(solution)/shard_map/ppermute | solution.py:152
  399.4 17.3 %collective-permute-start.19 = (bf16[576,2048]{1,0:T(8,128)(2,1)S(1)}, bf16[576,2048]{1,0:T(8,128)(2,1)S(1)}, u32[]{:S(2)}, u32[]{:S(2)}) collective-permute-start(bf16[576,2048]{1,0:T(8,128)(2,1)S(1)} %pad_maximum_fusion.8), channel_id=1, source_target_pairs={{4,0},{0,4},{5,1},{1,5},{6,2},{2,6},{7,3},{3,7},{12,8},{8,12},{13,... | collective-permute-start | bytes 7077896 | tf_op jit(solution)/shard_map/ppermute | solution.py:154
  415.1 4.7 collective-permute-start.9
  419.8 12.7 %copy-start.52 = (bf16[288,2048]{1,0:T(8,128)(2,1)S(1)}, bf16[288,2048]{1,0:T(8,128)(2,1)}, u32[]{:S(2)}) copy-start(bf16[288,2048]{1,0:T(8,128)(2,1)} %copy-done.51) | copy-start | bytes 3538948
  419.8 12.7 %copy-start.94 = (bf16[2048,3072]{0,1:T(8,128)(2,1)S(1)}, bf16[2048,3072]{0,1:T(8,128)(2,1)}, u32[]{:S(2)}) copy-start(bf16[2048,3072]{0,1:T(8,128)(2,1)} %all-gather.7.cloned.1.call-done) | copy-start | bytes 37748740
  485.0 14.9 %collective-permute-start.20 = (bf16[576,2048]{1,0:T(8,128)(2,1)S(1)}, bf16[576,2048]{1,0:T(8,128)(2,1)S(1)}, u32[]{:S(2)}, u32[]{:S(2)}) collective-permute-start(bf16[576,2048]{1,0:T(8,128)(2,1)S(1)} %slice.345), channel_id=1, source_target_pairs={{4,0},{0,4},{5,1},{1,5},{6,2},{2,6},{7,3},{3,7},{12,8},{8,12},{13,... | collective-permute-start | bytes 7077896 | tf_op jit(solution)/shard_map/ppermute | solution.py:161
  499.6 4.6 collective-permute-start.14
  503.1 28.9 %collective-permute-start.21 = (bf16[288,2048]{1,0:T(8,128)(2,1)S(1)}, bf16[288,2048]{1,0:T(8,128)(2,1)S(1)}, u32[]{:S(2)}, u32[]{:S(2)}) collective-permute-start(bf16[288,2048]{1,0:T(8,128)(2,1)S(1)} %slice.349), channel_id=1, source_target_pairs={{1,0},{0,1},{3,2},{2,3},{5,4},{4,5},{7,6},{6,7},{9,8},{8,9},{11,10... | collective-permute-start | bytes 3538952 | tf_op jit(solution)/shard_map/ppermute | solution.py:166
  505.5 51.2 %collective-permute-start.15 = (bf16[288,2048]{1,0:T(8,128)(2,1)S(1)}, bf16[288,2048]{1,0:T(8,128)(2,1)S(1)}, u32[]{:S(2)}, u32[]{:S(2)}) collective-permute-start(bf16[288,2048]{1,0:T(8,128)(2,1)S(1)} %slice.350), channel_id=1, source_target_pairs={{1,0},{0,1},{3,2},{2,3},{5,4},{4,5},{7,6},{6,7},{9,8},{8,9},{11,10... | collective-permute-start | bytes 3538952 | tf_op jit(solution)/shard_map/ppermute | solution.py:166
  561.1 43.2 %copy-start.37 = (bf16[288,2048]{1,0:T(8,128)(2,1)}, bf16[288,2048]{1,0:T(8,128)(2,1)S(1)}, u32[]{:S(2)}) copy-start(bf16[288,2048]{1,0:T(8,128)(2,1)S(1)} %get-tuple-element.446) | copy-start | bytes 3538948
  561.1 27.4 %collective-permute-start.22 = (bf16[288,2048]{1,0:T(8,128)(2,1)S(1)}, bf16[288,2048]{1,0:T(8,128)(2,1)S(1)}, u32[]{:S(2)}, u32[]{:S(2)}) collective-permute-start(bf16[288,2048]{1,0:T(8,128)(2,1)S(1)} %get-tuple-element.446), channel_id=1, source_target_pairs={{1,0},{0,1},{3,2},{2,3},{5,4},{4,5},{7,6},{6,7},{9,8},{8,9},{11,10... | collective-permute-start | bytes 3538952 | tf_op jit(solution)/shard_map/ppermute | solution.py:152
  591.2 13.2 %collective-permute-start.23 = (bf16[576,2048]{1,0:T(8,128)(2,1)}, bf16[576,2048]{1,0:T(8,128)(2,1)}, u32[]{:S(2)}, u32[]{:S(2)}) collective-permute-start(bf16[576,2048]{1,0:T(8,128)(2,1)} %pad_maximum_fusion.9), channel_id=1, source_target_pairs={{4,0},{0,4},{5,1},{1,5},{6,2},{2,6},{7,3},{3,7},{12,8},{8,12},{13,... | collective-permute-start | bytes 7077896 | tf_op jit(solution)/shard_map/ppermute | solution.py:154
  604.3 270.4 %reduce-scatter.4.cloned.1.call-start = ((), (), s32[]{:S(2)}) async-start(), calls=%async_computation.6 | async-start | bytes 7864320 | tf_op jit(solution)/shard_map/reduce_scatter | solution.py:184
  710.9 194.1 %reduce-scatter.6.cloned.1.call-start = ((), (), s32[]{:S(2)}) async-start(), calls=%async_computation.7 | async-start | bytes 15728640 | tf_op jit(solution)/shard_map/reduce_scatter | solution.py:184
  712.5 11.2 %copy-start.97 = (bf16[1152,1536]{1,0:T(8,128)(2,1)S(1)}, bf16[1152,1536]{1,0:T(8,128)(2,1)}, u32[]{:S(2)}) copy-start(bf16[1152,1536]{1,0:T(8,128)(2,1)} %get-tuple-element.460) | copy-start | bytes 10616836
  760.5 4.6 collective-permute-start.24
  760.8 9.6 collective-permute-start.16
  768.4 42.0 %copy-start.9 = (bf16[288,2048]{1,0:T(8,128)(2,1)S(1)}, bf16[288,2048]{1,0:T(8,128)(2,1)}, u32[]{:S(2)}) copy-start(bf16[288,2048]{1,0:T(8,128)(2,1)} %copy-done.7) | copy-start | bytes 3538948
  768.4 42.0 %copy-start.72 = (f32[1,2,8,128]{3,1,2,0:T(2,128)S(1)}, f32[1,2,8,128]{3,1,2,0:T(2,128)}, u32[]{:S(2)}) copy-start(f32[1,2,8,128]{3,1,2,0:T(2,128)} %copy-done.71) | copy-start | bytes 24580
  768.4 42.0 %copy-start.81 = (f32[288]{0:T(512)S(1)}, f32[288]{0:T(512)}, u32[]{:S(2)}) copy-start(f32[288]{0:T(512)} %copy-done.80) | copy-start | bytes 3460
  769.6 40.8 %collective-permute-start.25 = (bf16[288,2048]{1,0:T(8,128)(2,1)}, bf16[288,2048]{1,0:T(8,128)(2,1)S(1)}, u32[]{:S(2)}, u32[]{:S(2)}) collective-permute-start(bf16[288,2048]{1,0:T(8,128)(2,1)} %slice.348), channel_id=1, source_target_pairs={{1,0},{0,1},{3,2},{2,3},{5,4},{4,5},{7,6},{6,7},{9,8},{8,9},{11,10... | collective-permute-start | bytes 3538952 | tf_op jit(solution)/shard_map/ppermute | solution.py:166
  770.4 43.6 %copy-start.78 = (f32[2048]{0:T(1024)S(1)}, f32[2048]{0:T(1024)}, u32[]{:S(2)}) copy-start(f32[2048]{0:T(1024)} %get-tuple-element.388) | copy-start | bytes 24580
  770.4 43.6 %copy-start.88 = (f32[128]{0:T(128)S(1)}, f32[128]{0:T(128)}, u32[]{:S(2)}) copy-start(f32[128]{0:T(128)} %get-tuple-element.394) | copy-start | bytes 1540
  770.4 43.6 %copy-start.89 = (f32[128]{0:T(128)S(1)}, f32[128]{0:T(128)}, u32[]{:S(2)}) copy-start(f32[128]{0:T(128)} %get-tuple-element.392) | copy-start | bytes 1540
  770.4 84.2 %copy-start.83 = (f32[288]{0:T(512)S(1)}, f32[288]{0:T(512)}, u32[]{:S(2)}) copy-start(f32[288]{0:T(512)} %copy-done.82) | copy-start | bytes 3460
  770.4 43.5 %copy-start.43 = (bf16[288,2048]{1,0:T(8,128)(2,1)}, bf16[288,2048]{1,0:T(8,128)(2,1)S(1)}, u32[]{:S(2)}) copy-start(bf16[288,2048]{1,0:T(8,128)(2,1)S(1)} %collective-permute-done.16) | copy-start | bytes 3538948
  859.8 47.3 %collective-permute-start.26 = (bf16[288,2048]{1,0:T(8,128)(2,1)}, bf16[288,2048]{1,0:T(8,128)(2,1)}, u32[]{:S(2)}, u32[]{:S(2)}) collective-permute-start(bf16[288,2048]{1,0:T(8,128)(2,1)} %get-tuple-element.442), channel_id=1, source_target_pairs={{0,0},{2,4},{4,2},{6,6},{1,1},{3,5},{5,3},{7,7},{8,8},{10,12},{12,... | collective-permute-start | bytes 3538952 | tf_op jit(solution)/shard_map/ppermute | solution.py:147
  874.7 35.5 %collective-permute-start.31 = (bf16[256,1536]{0,1:T(8,128)(2,1)}, bf16[256,1536]{0,1:T(8,128)(2,1)S(1)}, u32[]{:S(2)}, u32[]{:S(2)}) collective-permute-start(bf16[256,1536]{0,1:T(8,128)(2,1)} %broadcast_select_fusion.13), channel_id=1, source_target_pairs={{4,0},{0,4},{5,1},{1,5},{6,2},{2,6},{7,3},{3,7},{12,8},{8,12},{13,... | collective-permute-start | bytes 2359304 | tf_op jit(solution)/shard_map/ppermute | solution.py:188
  877.3 36.5 %collective-permute-start.27 = (bf16[256,1536]{0,1:T(8,128)(2,1)}, bf16[256,1536]{0,1:T(8,128)(2,1)}, u32[]{:S(2)}, u32[]{:S(2)}) collective-permute-start(bf16[256,1536]{0,1:T(8,128)(2,1)} %broadcast_select_fusion.15), channel_id=1, source_target_pairs={{4,0},{0,4},{5,1},{1,5},{6,2},{2,6},{7,3},{3,7},{12,8},{8,12},{13,... | collective-permute-start | bytes 2359304 | tf_op jit(solution)/shard_map/ppermute | solution.py:188
  907.0 8.9 collective-permute-start.29
  911.2 88.8 %collective-permute-start.32 = (bf16[256,1536]{0,1:T(8,128)(2,1)S(1)}, bf16[256,1536]{0,1:T(8,128)(2,1)S(1)}, u32[]{:S(2)}, u32[]{:S(2)}) collective-permute-start(bf16[256,1536]{0,1:T(8,128)(2,1)S(1)} %broadcast_select_fusion.7), channel_id=1, source_target_pairs={{2,0},{0,2},{3,1},{1,3},{6,4},{4,6},{7,5},{5,7},{10,8},{8,10},{11,... | collective-permute-start | bytes 2359304 | tf_op jit(solution)/shard_map/ppermute | solution.py:190
  916.0 84.1 %copy-start.40 = (bf16[256,1536]{0,1:T(8,128)(2,1)S(1)}, bf16[256,1536]{0,1:T(8,128)(2,1)}, u32[]{:S(2)}) copy-start(bf16[256,1536]{0,1:T(8,128)(2,1)} %copy-done.39) | copy-start | bytes 2359300
  916.0 101.0 %collective-permute-start.28 = (bf16[256,1536]{0,1:T(8,128)(2,1)}, bf16[256,1536]{0,1:T(8,128)(2,1)}, u32[]{:S(2)}, u32[]{:S(2)}) collective-permute-start(bf16[256,1536]{0,1:T(8,128)(2,1)} %broadcast_select_fusion.8), channel_id=1, source_target_pairs={{2,0},{0,2},{3,1},{1,3},{6,4},{4,6},{7,5},{5,7},{10,8},{8,10},{11,... | collective-permute-start | bytes 2359304 | tf_op jit(solution)/shard_map/ppermute | solution.py:190
  917.7 132.5 %collective-permute-start.30 = (bf16[256,3072]{0,1:T(8,128)(2,1)}, bf16[256,3072]{0,1:T(8,128)(2,1)}, u32[]{:S(2)}, u32[]{:S(2)}) collective-permute-start(bf16[256,3072]{0,1:T(8,128)(2,1)} %broadcast_select_fusion), channel_id=1, source_target_pairs={{2,0},{0,2},{3,1},{1,3},{6,4},{4,6},{7,5},{5,7},{10,8},{8,10},{11,... | collective-permute-start | bytes 4718600 | tf_op jit(solution)/shard_map/ppermute | solution.py:190
  (79 other events, 227.9 us)
Sparse Core Ops, SparseCore 0:
  54.3 71.2 all-gather.4
  179.3 123.1 all-gather.6
  333.9 68.6 all-gather.8
  604.4 68.4 reduce-scatter.7
  711.0 68.9 reduce-scatter.3
  783.0 121.9 reduce-scatter.5
where the time goes:
time: 1070 us; the launch traced here: 1060 us
  waiting for transfers between devices  470 us (44%)
  matrix products  204 us (19%)
  local copies, waits for them, and re-layouts  134 us (13%)
  other arithmetic  119 us (11%)
  blocking collectives  65 us (6%)
  starting transfers between devices  55.5 us (5%)
  between operations  16.4 us (2%)
    ppermute x4, waiting for transfers between devices, scatter_tokens(): lax.ppermute(sent, 'l', shift_perm(places, -step)).astype(jnp.float32)  126 us
    ppermute x3, waiting for transfers between devices, gather_weights(): far = lax.ppermute(shard, 'h', shift_perm(2, 1))  122 us
    ppermute x3, waiting for transfers between devices, scatter_weights(): far = lax.ppermute(jnp.where(same, other, mine), 'h', shift_perm(2, 1))  113 us
    ppermute x4, waiting for transfers between devices, gather_tokens(): lax.ppermute(own, 'l', shift_perm(places, step))  74.4 us
    unnamed x210, local copies, waits for them, and re-layouts  51.2 us
    dot_general x7, matrix products, contract_rows(): lax.dot_general(left, right, (((0,), (0,)), ((), ())), preferred_element_...  50.7 us
    dot_general x7, matrix products, contract_cols(): lax.dot_general(left, right, (((1,), (1,)), ((), ())), preferred_element_...  46.3 us
    psum x1, blocking collectives, per_device(): lax.psum(jnp.concatenate([attn_gain_grad, mlp_gain_grad, q_gain_grad, k_g...  39.3 us
  transfers between devices with their start and end apart: 39, of which 19 were waited for; matrix products, arithmetic and copies ran while one was open for 34% of the time, Pallas kernels for 0%

commit v1 on v0

--- a/solution.py
+++ b/solution.py
@@ -339,9 +339,12 @@
     gradient = gradient + stream_grad
     moved = trade(gradient.astype(jnp.bfloat16))
     gradient = jnp.where(core == lax.axis_index("h"), gradient, moved.astype(jnp.float32))
-    sums = lax.psum(
-        jnp.concatenate([attn_gain_grad, mlp_gain_grad, q_gain_grad, k_gain_grad]),
-        ("d", "c", "h", "l"),
+    sums = jnp.sum(
+        lax.all_gather(
+            jnp.concatenate([attn_gain_grad, mlp_gain_grad, q_gain_grad, k_gain_grad]),
+            ("d", "c", "h", "l"),
+        ),
+        axis=0,
     )
     row = lax.axis_index("d") * 2 + core
 

time: 1070 us -> 1080 us (level)
  blocking collectives: 65 us -> 97.4 us
  waiting for transfers between devices: 470 us -> 441 us
    all_gather x0 -> x1, blocking collectives: none -> 71.7 us  [per_device(): lax.all_gather(jnp.concatenate([attn_gain_grad, mlp_gain_grad, q_gain_gra...]
    psum x1 -> x0, blocking collectives: 39.3 us -> none  [per_device(): lax.psum(jnp.concatenate([attn_gain_grad, mlp_gain_grad, q_gain_grad, k_g...]
    reduce_scatter x3, waiting for transfers between devices: 27.4 us -> 0.01 us  [scatter_weights(): lax.psum_scatter(partial.astype(jnp.bfloat16), 'd', scatter_dimension=0,...]
    unnamed x210 -> x211, local copies, waits for them, and re-layouts: 51.2 us -> 51.2 us
  transfers between devices with their start and end apart: 39 -> 39, of which waited for: 19 -> 18; matrix products, arithmetic and copies ran while one was open for 34% -> 33% of each run, Pallas kernels for 0% -> 0%
where the time goes in v1:
time: 1080 us; the launch traced here: 1070 us
  waiting for transfers between devices  441 us (41%)
  matrix products  204 us (19%)
  local copies, waits for them, and re-layouts  134 us (12%)
  other arithmetic  119 us (11%)
  blocking collectives  97.4 us (9%)
  starting transfers between devices  59.3 us (5%)
  between operations  16.5 us (2%)
    ppermute x4, waiting for transfers between devices, scatter_tokens(): lax.ppermute(sent, 'l', shift_perm(places, -step)).astype(jnp.float32)  126 us
    ppermute x3, waiting for transfers between devices, gather_weights(): far = lax.ppermute(shard, 'h', shift_perm(2, 1))  122 us
    ppermute x3, waiting for transfers between devices, scatter_weights(): far = lax.ppermute(jnp.where(same, other, mine), 'h', shift_perm(2, 1))  111 us
    ppermute x4, waiting for transfers between devices, gather_tokens(): lax.ppermute(own, 'l', shift_perm(places, step))  74.4 us
    all_gather x1, blocking collectives, per_device(): lax.all_gather(jnp.concatenate([attn_gain_grad, mlp_gain_grad, q_gain_gra...  71.7 us
    unnamed x211, local copies, waits for them, and re-layouts  51.2 us
    dot_general x7, matrix products, contract_rows(): lax.dot_general(left, right, (((0,), (0,)), ((), ())), preferred_element_...  50.7 us
    dot_general x7, matrix products, contract_cols(): lax.dot_general(left, right, (((1,), (1,)), ((), ())), preferred_element_...  46.3 us
  transfers between devices with their start and end apart: 39, of which 18 were waited for; matrix products, arithmetic and copies ran while one was open for 33% of the time, Pallas kernels for 0%

profile of v1, /device:TPU:0, one launch (start us, length us, event | category | flops | bytes accessed | tf_op | source)
XLA Modules:
  0.0 1071.7 jit_solution(17313919162058695017)
XLA Ops:
  11.5 4.1 collective-permute-start.4
  15.6 34.4 %collective-permute-done.4 = bf16[256,1536]{0,1:T(8,128)(2,1)S(1)} collective-permute-done((bf16[256,1536]{0,1:T(8,128)(2,1)S(1)}, bf16[256,1536]{0,1:T(8,128)(2,1)S(1)}, u32[]{:S(2)}, u32[]{:S(2)}) %collective-permute-start.4) | collective-permute-done | bytes 786464 | tf_op jit(solution)/shard_map/ppermute | solution.py:172
  59.5 3.3 collective-permute-start.10
  64.4 25.7 %all-reduce.4 = bf16[4352]{0:T(1024)(128)(2,1)S(1)} all-reduce(bf16[4352]{0:T(1024)(128)(2,1)S(1)} %dynamic-update-slice), channel_id=2, replica_groups=mesh['d'=4,'c'=2,'h'=2,'l'=2] {'d','c'}, use_global_device_ids=true, to_apply=%add.4 | all-reduce | flops 4352 | bytes 17408
  102.3 51.4 %collective-permute-done.10 = bf16[256,3072]{0,1:T(8,128)(2,1)} collective-permute-done((bf16[256,3072]{0,1:T(8,128)(2,1)}, bf16[256,3072]{0,1:T(8,128)(2,1)}, u32[]{:S(2)}, u32[]{:S(2)}) %collective-permute-start.10) | collective-permute-done | bytes 1572896 | tf_op jit(solution)/shard_map/ppermute | solution.py:172
  155.6 9.9 collective-permute-done.2
  167.3 6.5 collective-permute-start.3
  180.8 3.5 multiply_reduce_fusion.8
  186.1 7.4 multiply_reduce_fusion.5
  200.7 3.8 copy.230
  204.5 5.0 copy.228
  210.8 7.0 fusion.70
  219.4 4.4 convolution_convert_fusion.8
  225.2 25.8 %while.28 = (s32[]{:T(128)}, bf16[2,576,2,2,128]{4,3,2,1,0:T(2,128)(2,1)S(1)}, f32[2,2,2,576,1]{3,2,1,4,0:T(2,128)}, s32[2,576]{1,0:T(2,128)}, s32[4,288]{1,0:T(...) while((s32[]{:T(128)}, ...), condition=%wide.region_7.8_spmd.clone, body=%wide.region_5.7_spmd.clone.sunk | while | flops 1379818368 | bytes 26884800 | solution.py:90
  230.6 3.1 bitcast_reduce_fusion.2
  233.7 3.1 fusion.140
  243.5 3.1 bitcast_reduce_fusion.2
  246.6 3.1 fusion.140
  252.1 15.6 %reshape.558 = bf16[1152,512]{1,0:T(8,128)(2,1)S(1)} reshape(bf16[2,576,2,2,128]{4,3,2,1,0:T(2,128)(2,1)} %copy-done.46) | data formatting | bytes 2359296 | tf_op jit(solution)/shard_map/reshape | solution.py:91
  267.7 4.6 fusion.72
  279.7 36.7 %collective-permute-done.12 = bf16[256,1536]{0,1:T(8,128)(2,1)S(1)} collective-permute-done((bf16[256,1536]{0,1:T(8,128)(2,1)S(1)}, bf16[256,1536]{0,1:T(8,128)(2,1)S(1)}, u32[]{:S(2)}, u32[]{:S(2)}) %collective-permute-start.12) | collective-permute-done | bytes 786464 | tf_op jit(solution)/shard_map/ppermute | solution.py:172
  316.6 10.4 collective-permute-start.17
  335.1 37.7 %collective-permute-done.7 = bf16[288,2048]{1,0:T(8,128)(2,1)} collective-permute-done((bf16[288,2048]{1,0:T(8,128)(2,1)}, bf16[288,2048]{1,0:T(8,128)(2,1)}, u32[]{:S(2)}, u32[]{:S(2)}) %collective-permute-start.7) | collective-permute-done | bytes 1179680 | tf_op jit(solution)/shard_map/ppermute | solution.py:166
  375.8 22.1 %collective-permute-done.18 = bf16[288,2048]{1,0:T(8,128)(2,1)S(1)} collective-permute-done((bf16[288,2048]{1,0:T(8,128)(2,1)}, bf16[288,2048]{1,0:T(8,128)(2,1)S(1)}, u32[]{:S(2)}, u32[]{:S(2)}) %collective-permute-start.18) | collective-permute-done | bytes 1179680 | tf_op jit(solution)/shard_map/ppermute | solution.py:152
  399.5 15.3 %collective-permute-done.8 = bf16[288,2048]{1,0:T(8,128)(2,1)S(1)} collective-permute-done((bf16[288,2048]{1,0:T(8,128)(2,1)S(1)}, bf16[288,2048]{1,0:T(8,128)(2,1)S(1)}, u32[]{:S(2)}, u32[]{:S(2)}) %collective-permute-start.8) | collective-permute-done | bytes 1179680 | tf_op jit(solution)/shard_map/ppermute | solution.py:152
  419.8 12.7 %fusion.52 = f32[1152,1536]{1,0:T(8,128)} fusion(bf16[2048,3072]{0,1:T(8,128)(2,1)} %all-gather.9.cloned.1.call-done, bf16[576,2048]{1,0:T(8,128)(2,1)} %collective-permute-done.9, bf16[288,2048]{1,0:T(8,128)(2,1)} %copy-done.51, bf16[288,2048]{1,0:T(8,128)(2,1)S(1)} %multiply_convert_fusion.2), kind=kOutput, calls=%fused_computation.75 | convolution fusion | flops 7261913088 | bytes 18087936 | tf_op jit(solution)/shard_map/dot_general | solution.py:271
  432.6 11.0 %fusion.56 = f32[1152,1536]{1,0:T(8,128)} fusion(bf16[2048,3072]{0,1:T(8,128)(2,1)S(1)} %copy-done.94, bf16[576,2048]{1,0:T(8,128)(2,1)} %collective-permute-done.9, bf16[288,2048]{1,0:T(8,128)(2,1)S(1)} %copy-done.52, bf16[288,2048]{1,0:T(8,128)(2,1)S(1)} %multiply_convert_fusion.2), kind=kOutput, calls=%fused_computation.79 | convolution fusion | flops 7261913088 | bytes 18087936 | tf_op jit(solution)/shard_map/dot_general | solution.py:270
  443.5 18.9 %multiply_convert_fusion = (bf16[1152,1536]{1,0:T(8,128)(2,1)}, bf16[1152,1536]{1,0:T(8,128)(2,1)}, bf16[1152,1536]{1,0:T(8,128)(2,1)}) fusion(f32[1152,1536]{1,0:T(8,128)} %fusion.56, f32[1152,1536]{1,0:T(8,128)} %fusion.52, bf16[1152,2048]{1,0:T(8,128)(2,1)} %copy-done.64, bf16[2048,1536]{0,1:T(8,128)(2,1)} %all-gather.11.cloned.1.call-done), kind=kOutput, calls=%fused_computation.69 | convolution fusion | flops 7276068864 | bytes 35782656 | tf_op jit(solution)/shard_map/dot_general | solution.py:278
  462.5 11.2 %fusion.54 = f32[1152,2048]{1,0:T(8,128)S(1)} fusion(bf16[1152,1536]{1,0:T(8,128)(2,1)} %get-tuple-element.497, bf16[2048,3072]{0,1:T(8,128)(2,1)} %all-gather.9.cloned.1.call-done), kind=kOutput, calls=%fused_computation.77 | convolution fusion | flops 7247757312 | bytes 19267584 | tf_op jit(solution)/shard_map/dot_general | solution.py:50
  473.7 10.9 %convolution_add_fusion.2 = f32[1152,2048]{1,0:T(8,128)S(1)} fusion(f32[1152,2048]{1,0:T(8,128)S(1)} %fusion.54, bf16[1152,1536]{1,0:T(8,128)(2,1)} %get-tuple-element.496, bf16[2048,3072]{0,1:T(8,128)(2,1)} %all-gather.9.cloned.1.call-done), kind=kOutput, calls=%fused_computation.62 | convolution fusion | flops 7250116608 | bytes 28704768 | tf_op jit(solution)/shard_map/dot_general | solution.py:50
  485.2 3.8 copy-done.29
  489.3 10.0 fusion.102
  499.9 3.1 slice_add_fusion.1
  506.5 25.5 %collective-permute-done.21 = bf16[288,2048]{1,0:T(8,128)(2,1)S(1)} collective-permute-done((bf16[288,2048]{1,0:T(8,128)(2,1)S(1)}, bf16[288,2048]{1,0:T(8,128)(2,1)S(1)}, u32[]{:S(2)}, u32[]{:S(2)}) %collective-permute-start.21) | collective-permute-done | bytes 1179680 | tf_op jit(solution)/shard_map/ppermute | solution.py:166
  533.4 23.3 %collective-permute-done.15 = bf16[288,2048]{1,0:T(8,128)(2,1)S(1)} collective-permute-done((bf16[288,2048]{1,0:T(8,128)(2,1)S(1)}, bf16[288,2048]{1,0:T(8,128)(2,1)S(1)}, u32[]{:S(2)}, u32[]{:S(2)}) %collective-permute-start.15) | collective-permute-done | bytes 1179680 | tf_op jit(solution)/shard_map/ppermute | solution.py:166
  556.7 4.4 fusion.95
  561.4 27.1 %collective-permute-done.22 = bf16[288,2048]{1,0:T(8,128)(2,1)S(1)} collective-permute-done((bf16[288,2048]{1,0:T(8,128)(2,1)S(1)}, bf16[288,2048]{1,0:T(8,128)(2,1)S(1)}, u32[]{:S(2)}, u32[]{:S(2)}) %collective-permute-start.22) | collective-permute-done | bytes 1179680 | tf_op jit(solution)/shard_map/ppermute | solution.py:152
  591.2 13.1 %convolution_convert_fusion = bf16[2048,1536]{0,1:T(8,128)(2,1)} fusion(bf16[1152,2048]{1,0:T(8,128)(2,1)} %copy-done.64, bf16[1152,1536]{1,0:T(8,128)(2,1)} %get-tuple-element.498), kind=kOutput, calls=%fused_computation.63 | convolution fusion | flops 7250903040 | bytes 14548992 | tf_op jit(solution)/shard_map/dot_general | solution.py:44
  604.4 6.3 convolution_convert_fusion.5
  610.7 3.8 reshape_reshape.5
  614.5 55.6 %while.29 = (s32[]{:T(128)}, f32[1152,2,128]{0,2,1:T(8,128)S(1)}, f32[1152,2,128]{0,2,1:T(8,128)S(1)}, f32[2,576,2,2,128]{4,1,0,3,2:T(8,128)}, bf16[2,576,2,2,12...) while((s32[]{:T(128)}, f32[1152,2,128]{0,2,1:T(8,128)S(1)}, ...), condition=%wide.region_12.13_spmd.clone, body=%wide.region_10.12_spmd.clone.sunk | while | flops 3425033216 | bytes 203141424 | solution.py:136
  622.2 4.0 fusion.148
  635.1 4.2 fusion.150
  649.7 4.0 fusion.148
  662.7 4.4 fusion.150
  670.1 3.3 copy.211
  681.6 3.2 convolution_convert_fusion.7
  684.8 3.4 convolution_convert_fusion.6
  688.2 4.7 convolution_convert_fusion.4
  693.4 5.0 convolution_convert_fusion.3
  698.5 12.4 %pad_maximum_fusion.1 = bf16[2048,1536]{0,1:T(8,128)(2,1)} fusion(bf16[2048,512]{0,1:T(8,128)(2,1)S(1)} %convolution_convert_fusion.4, bf16[2048,256]{0,1:T(8,128)(2,1)S(1)} %convolution_convert_fusion.6, bf16[2048,256]{0,1:T(8,128)(2,1)S(1)} %convolution_convert_fusion.7, bf16[2048,512]{0,1:T(8,128)(2,1)S(1)} %convolution_convert_fusion.3), kind=kLoop, calls=%fused_computation.73 | loop fusion | flops 25165824 | bytes 12582912 | tf_op jit(solution)/shard_map/concatenate | solution.py:322
  712.5 11.2 %convolution_convert_fusion.2 = bf16[2048,1536]{0,1:T(8,128)(2,1)S(1)} fusion(bf16[1152,1536]{1,0:T(8,128)(2,1)} %get-tuple-element.497, bf16[576,2048]{1,0:T(8,128)(2,1)} %collective-permute-done.9, bf16[288,2048]{1,0:T(8,128)(2,1)S(1)} %copy-done.53, bf16[288,2048]{1,0:T(8,128)(2,1)S(1)} %copy-done.31), kind=kOutput, calls=%fused_computation.65 | convolution fusion | flops 7265058816 | bytes 14548992 | tf_op jit(solution)/shard_map/dot_general | solution.py:44
  723.7 10.2 convolution_convert_fusion.1
  733.9 15.3 %pad_maximum_fusion = bf16[2048,3072]{0,1:T(8,128)(2,1)} fusion(bf16[2048,1536]{0,1:T(8,128)(2,1)S(1)} %convolution_convert_fusion.1, bf16[2048,1536]{0,1:T(8,128)(2,1)S(1)} %convolution_convert_fusion.2), kind=kLoop, calls=%fused_computation.58 | loop fusion | flops 25165824 | bytes 25165824 | tf_op jit(solution)/shard_map/concatenate | solution.py:284
  750.6 4.2 fusion.74
  770.4 39.9 %collective-permute-done.25 = bf16[288,2048]{1,0:T(8,128)(2,1)S(1)} collective-permute-done((bf16[288,2048]{1,0:T(8,128)(2,1)}, bf16[288,2048]{1,0:T(8,128)(2,1)S(1)}, u32[]{:S(2)}, u32[]{:S(2)}) %collective-permute-start.25) | collective-permute-done | bytes 1179680 | tf_op jit(solution)/shard_map/ppermute | solution.py:166
  810.4 3.6 fusion.61
  814.0 71.7 %all-gather.2 = f32[32,1,4352]{2,1,0:T(1,128)S(1)} all-gather(f32[1,1,4352]{2,1,0:T(1,128)S(1)} %reshape.574), channel_id=3, replica_groups=mesh['d'=4,'c'=2,'h'=2,'l'=2] {'d','c','h','l'}, dimensions={0}, use_global_device_ids=true | all-gather | bytes 574464 | tf_op jit(solution)/shard_map/all_gather | solution.py:343
  888.0 5.0 fusion.93
  893.0 10.5 collective-permute-start.26
  917.0 6.2 collective-permute-start.32
  930.0 77.4 %collective-permute-done.32 = bf16[256,1536]{0,1:T(8,128)(2,1)S(1)} collective-permute-done((bf16[256,1536]{0,1:T(8,128)(2,1)S(1)}, bf16[256,1536]{0,1:T(8,128)(2,1)S(1)}, u32[]{:S(2)}, u32[]{:S(2)}) %collective-permute-start.32) | collective-permute-done | bytes 786464 | tf_op jit(solution)/shard_map/ppermute | solution.py:190
  1011.9 12.4 %collective-permute-done.28 = bf16[256,1536]{0,1:T(8,128)(2,1)} collective-permute-done((bf16[256,1536]{0,1:T(8,128)(2,1)}, bf16[256,1536]{0,1:T(8,128)(2,1)}, u32[]{:S(2)}, u32[]{:S(2)}) %collective-permute-start.28) | collective-permute-done | bytes 786464 | tf_op jit(solution)/shard_map/ppermute | solution.py:190
  1036.9 21.1 %collective-permute-done.30 = bf16[256,3072]{0,1:T(8,128)(2,1)} collective-permute-done((bf16[256,3072]{0,1:T(8,128)(2,1)}, bf16[256,3072]{0,1:T(8,128)(2,1)}, u32[]{:S(2)}, u32[]{:S(2)}) %collective-permute-start.30) | collective-permute-done | bytes 1572896 | tf_op jit(solution)/shard_map/ppermute | solution.py:190
  (460 shorter events, 210.7 us)
Async XLA Ops:
  7.2 172.5 %all-gather.7.cloned.1.call-start = ((), (), s32[]{:S(2)}) async-start(), calls=%async_computation.3 | async-start | bytes 7864320 | tf_op jit(solution)/shard_map/all_gather | solution.py:179
  11.5 38.5 %collective-permute-start.4 = (bf16[256,1536]{0,1:T(8,128)(2,1)S(1)}, bf16[256,1536]{0,1:T(8,128)(2,1)S(1)}, u32[]{:S(2)}, u32[]{:S(2)}) collective-permute-start(bf16[256,1536]{0,1:T(8,128)(2,1)S(1)} %pad_maximum_fusion.15), channel_id=1, source_target_pairs={{2,0},{0,2},{3,1},{1,3},{6,4},{4,6},{7,5},{5,7},{10,8},{8,10},{11,... | collective-permute-start | bytes 2359304 | tf_op jit(solution)/shard_map/ppermute | solution.py:172
  50.2 2.4 collective-permute-start.5
  54.2 365.6 %all-gather.9.cloned.1.call-start = ((), (), s32[]{:S(2)}) async-start(), calls=%async_computation.4 | async-start | bytes 15728640 | tf_op jit(solution)/shard_map/all_gather | solution.py:179
  54.3 42.5 %collective-permute-start = (bf16[288,2048]{1,0:T(8,128)(2,1)}, bf16[288,2048]{1,0:T(8,128)(2,1)S(1)}, u32[]{:S(2)}, u32[]{:S(2)}) collective-permute-start(bf16[288,2048]{1,0:T(8,128)(2,1)} %param.18), channel_id=1, source_target_pairs={{0,0},{2,4},{4,2},{6,6},{1,1},{3,5},{5,3},{7,7},{8,8},{10,12},{12,... | collective-permute-start | bytes 3538952 | tf_op jit(solution)/shard_map/ppermute | solution.py:147
  56.3 38.7 %collective-permute-start.1 = (s32[1,1152]{1,0:T(1,128)}, s32[1,1152]{1,0:T(1,128)S(1)}, u32[]{:S(2)}, u32[]{:S(2)}) collective-permute-start(s32[1,1152]{1,0:T(1,128)} %param.19), channel_id=1, source_target_pairs={{0,0},{2,4},{4,2},{6,6},{1,1},{3,5},{5,3},{7,7},{8,8},{10,12},{12,... | collective-permute-start | bytes 13832 | tf_op jit(solution)/shard_map/ppermute | solution.py:147
  59.5 94.2 %collective-permute-start.10 = (bf16[256,3072]{0,1:T(8,128)(2,1)}, bf16[256,3072]{0,1:T(8,128)(2,1)}, u32[]{:S(2)}, u32[]{:S(2)}) collective-permute-start(bf16[256,3072]{0,1:T(8,128)(2,1)} %pad_maximum_fusion.13), channel_id=1, source_target_pairs={{2,0},{0,2},{3,1},{1,3},{6,4},{4,6},{7,5},{5,7},{10,8},{8,10},{11,... | collective-permute-start | bytes 4718600 | tf_op jit(solution)/shard_map/ppermute | solution.py:172
  97.1 58.4 %copy-start.82 = (f32[288]{0:T(512)}, f32[288]{0:T(512)S(1)}, u32[]{:S(2)}) copy-start(f32[288]{0:T(512)S(1)} %fusion.65) | copy-start | bytes 3460
  97.1 58.4 %copy-start.80 = (f32[288]{0:T(512)}, f32[288]{0:T(512)S(1)}, u32[]{:S(2)}) copy-start(f32[288]{0:T(512)S(1)} %fusion.88) | copy-start | bytes 3460
  97.4 68.1 %copy-start.32 = (bf16[288,2048]{1,0:T(8,128)(2,1)}, bf16[288,2048]{1,0:T(8,128)(2,1)S(1)}, u32[]{:S(2)}) copy-start(bf16[288,2048]{1,0:T(8,128)(2,1)S(1)} %fusion.60) | copy-start | bytes 3538948
  97.4 68.0 %collective-permute-start.2 = (bf16[288,2048]{1,0:T(8,128)(2,1)S(1)}, bf16[288,2048]{1,0:T(8,128)(2,1)S(1)}, u32[]{:S(2)}, u32[]{:S(2)}) collective-permute-start(bf16[288,2048]{1,0:T(8,128)(2,1)S(1)} %fusion.60), channel_id=1, source_target_pairs={{1,0},{0,1},{3,2},{2,3},{5,4},{4,5},{7,6},{6,7},{9,8},{8,9},{11,10... | collective-permute-start | bytes 3538952 | tf_op jit(solution)/shard_map/ppermute | solution.py:152
  155.5 20.9 %collective-permute-start.11 = (bf16[256,3072]{0,1:T(8,128)(2,1)S(1)}, bf16[256,3072]{0,1:T(8,128)(2,1)S(1)}, u32[]{:S(2)}, u32[]{:S(2)}) collective-permute-start(bf16[256,3072]{0,1:T(8,128)(2,1)S(1)} %broadcast_select_fusion.1), channel_id=1, source_target_pairs={{4,0},{0,4},{5,1},{1,5},{6,2},{2,6},{7,3},{3,7},{12,8},{8,12},{13,... | collective-permute-start | bytes 4718600 | tf_op jit(solution)/shard_map/ppermute | solution.py:175
  167.3 12.3 %collective-permute-start.3 = (bf16[576,2048]{1,0:T(8,128)(2,1)}, bf16[576,2048]{1,0:T(8,128)(2,1)}, u32[]{:S(2)}, u32[]{:S(2)}) collective-permute-start(bf16[576,2048]{1,0:T(8,128)(2,1)} %pad_maximum_fusion.6), channel_id=1, source_target_pairs={{4,0},{0,4},{5,1},{1,5},{6,2},{2,6},{7,3},{3,7},{12,8},{8,12},{13,... | collective-permute-start | bytes 7077896 | tf_op jit(solution)/shard_map/ppermute | solution.py:154
  176.3 9.0 copy-start.22
  176.4 9.0 copy-start.24
  179.2 264.3 %all-gather.11.cloned.1.call-start = ((), (), s32[]{:S(2)}) async-start(), calls=%async_computation.5 | async-start | bytes 7864320 | tf_op jit(solution)/shard_map/all_gather | solution.py:179
  252.0 20.3 %copy-start.12 = (bf16[1152,2,128]{2,0,1:T(8,128)(2,1)}, bf16[1152,2,128]{2,0,1:T(8,128)(2,1)S(1)}, u32[]{:S(2)}) copy-start(bf16[1152,2,128]{2,0,1:T(8,128)(2,1)S(1)} %get-tuple-element.810) | copy-start | bytes 1769476
  252.0 20.3 %copy-start.14 = (bf16[1152,2,128]{2,0,1:T(8,128)(2,1)}, bf16[1152,2,128]{2,0,1:T(8,128)(2,1)S(1)}, u32[]{:S(2)}) copy-start(bf16[1152,2,128]{2,0,1:T(8,128)(2,1)S(1)} %get-tuple-element.811) | copy-start | bytes 1769476
  252.0 20.3 %copy-start.16 = (bf16[2,576,2,2,128]{4,1,3,2,0:T(8,128)(2,1)}, bf16[2,576,2,2,128]{4,1,3,2,0:T(8,128)(2,1)S(1)}, u32[]{:S(2)}) copy-start(bf16[2,576,2,2,128]{4,1,3,2,0:T(8,128)(2,1)S(1)} %get-tuple-element.812) | copy-start | bytes 3538948
  252.0 20.3 %copy-start.58 = (s32[4,288]{1,0:T(4,128)}, s32[4,288]{1,0:T(4,128)S(1)}, u32[]{:S(2)}) copy-start(s32[4,288]{1,0:T(4,128)S(1)} %get-tuple-element.854) | copy-start | bytes 13828
  252.0 20.4 %copy-start.69 = (s32[2,576]{1,0:T(2,128)}, s32[2,576]{1,0:T(2,128)S(1)}, u32[]{:S(2)}) copy-start(s32[2,576]{1,0:T(2,128)S(1)} %get-tuple-element.863) | copy-start | bytes 13828
  276.7 50.3 %collective-permute-start.6 = (bf16[576,2048]{1,0:T(8,128)(2,1)}, bf16[576,2048]{1,0:T(8,128)(2,1)S(1)}, u32[]{:S(2)}, u32[]{:S(2)}) collective-permute-start(bf16[576,2048]{1,0:T(8,128)(2,1)} %slice.347), channel_id=1, source_target_pairs={{4,0},{0,4},{5,1},{1,5},{6,2},{2,6},{7,3},{3,7},{12,8},{8,12},{13,... | collective-permute-start | bytes 7077896 | tf_op jit(solution)/shard_map/ppermute | solution.py:161
  279.7 36.7 %collective-permute-start.12 = (bf16[256,1536]{0,1:T(8,128)(2,1)S(1)}, bf16[256,1536]{0,1:T(8,128)(2,1)S(1)}, u32[]{:S(2)}, u32[]{:S(2)}) collective-permute-start(bf16[256,1536]{0,1:T(8,128)(2,1)S(1)} %bitcast.247), channel_id=1, source_target_pairs={{2,0},{0,2},{3,1},{1,3},{6,4},{4,6},{7,5},{5,7},{10,8},{8,10},{11,... | collective-permute-start | bytes 2359304 | tf_op jit(solution)/shard_map/ppermute | solution.py:172
  316.5 14.9 %collective-permute-start.13 = (bf16[256,1536]{0,1:T(8,128)(2,1)S(1)}, bf16[256,1536]{0,1:T(8,128)(2,1)S(1)}, u32[]{:S(2)}, u32[]{:S(2)}) collective-permute-start(bf16[256,1536]{0,1:T(8,128)(2,1)S(1)} %broadcast_select_fusion.9), channel_id=1, source_target_pairs={{4,0},{0,4},{5,1},{1,5},{6,2},{2,6},{7,3},{3,7},{12,8},{8,12},{13,... | collective-permute-start | bytes 2359304 | tf_op jit(solution)/shard_map/ppermute | solution.py:175
  316.6 17.3 %collective-permute-start.17 = (bf16[288,2048]{1,0:T(8,128)(2,1)}, bf16[288,2048]{1,0:T(8,128)(2,1)}, u32[]{:S(2)}, u32[]{:S(2)}) collective-permute-start(bf16[288,2048]{1,0:T(8,128)(2,1)} %param.31), channel_id=1, source_target_pairs={{0,0},{2,4},{4,2},{6,6},{1,1},{3,5},{5,3},{7,7},{8,8},{10,12},{12,... | collective-permute-start | bytes 3538952 | tf_op jit(solution)/shard_map/ppermute | solution.py:147
  331.4 41.4 %collective-permute-start.7 = (bf16[288,2048]{1,0:T(8,128)(2,1)}, bf16[288,2048]{1,0:T(8,128)(2,1)}, u32[]{:S(2)}, u32[]{:S(2)}) collective-permute-start(bf16[288,2048]{1,0:T(8,128)(2,1)} %slice.351), channel_id=1, source_target_pairs={{1,0},{0,1},{3,2},{2,3},{5,4},{4,5},{7,6},{6,7},{9,8},{8,9},{11,10... | collective-permute-start | bytes 3538952 | tf_op jit(solution)/shard_map/ppermute | solution.py:166
  332.5 40.3 %copy-start.8 = (bf16[288,2048]{1,0:T(8,128)(2,1)S(1)}, bf16[288,2048]{1,0:T(8,128)(2,1)}, u32[]{:S(2)}) copy-start(bf16[288,2048]{1,0:T(8,128)(2,1)} %copy-done.7) | copy-start | bytes 3538948
  333.8 571.7 %reduce-scatter.8.cloned.1.call-start = ((), (), s32[]{:S(2)}) async-start(), calls=%async_computation.8 | async-start | bytes 7864320 | tf_op jit(solution)/shard_map/reduce_scatter | solution.py:184
  333.9 64.0 %collective-permute-start.18 = (bf16[288,2048]{1,0:T(8,128)(2,1)}, bf16[288,2048]{1,0:T(8,128)(2,1)S(1)}, u32[]{:S(2)}, u32[]{:S(2)}) collective-permute-start(bf16[288,2048]{1,0:T(8,128)(2,1)} %collective-permute-done.17), channel_id=1, source_target_pairs={{1,0},{0,1},{3,2},{2,3},{5,4},{4,5},{7,6},{6,7},{9,8},{8,9},{11,10... | collective-permute-start | bytes 3538952 | tf_op jit(solution)/shard_map/ppermute | solution.py:152
  375.7 56.8 %copy-start.30 = (bf16[288,2048]{1,0:T(8,128)(2,1)}, bf16[288,2048]{1,0:T(8,128)(2,1)S(1)}, u32[]{:S(2)}) copy-start(bf16[288,2048]{1,0:T(8,128)(2,1)S(1)} %multiply_convert_fusion.2) | copy-start | bytes 3538948
  375.8 39.0 %collective-permute-start.8 = (bf16[288,2048]{1,0:T(8,128)(2,1)S(1)}, bf16[288,2048]{1,0:T(8,128)(2,1)S(1)}, u32[]{:S(2)}, u32[]{:S(2)}) collective-permute-start(bf16[288,2048]{1,0:T(8,128)(2,1)S(1)} %multiply_convert_fusion.2), channel_id=1, source_target_pairs={{1,0},{0,1},{3,2},{2,3},{5,4},{4,5},{7,6},{6,7},{9,8},{8,9},{11,10... | collective-permute-start | bytes 3538952 | tf_op jit(solution)/shard_map/ppermute | solution.py:152
  399.4 17.3 %collective-permute-start.19 = (bf16[576,2048]{1,0:T(8,128)(2,1)S(1)}, bf16[576,2048]{1,0:T(8,128)(2,1)S(1)}, u32[]{:S(2)}, u32[]{:S(2)}) collective-permute-start(bf16[576,2048]{1,0:T(8,128)(2,1)S(1)} %pad_maximum_fusion.8), channel_id=1, source_target_pairs={{4,0},{0,4},{5,1},{1,5},{6,2},{2,6},{7,3},{3,7},{12,8},{8,12},{13,... | collective-permute-start | bytes 7077896 | tf_op jit(solution)/shard_map/ppermute | solution.py:154
  415.1 4.7 collective-permute-start.9
  419.8 12.7 %copy-start.52 = (bf16[288,2048]{1,0:T(8,128)(2,1)S(1)}, bf16[288,2048]{1,0:T(8,128)(2,1)}, u32[]{:S(2)}) copy-start(bf16[288,2048]{1,0:T(8,128)(2,1)} %copy-done.51) | copy-start | bytes 3538948
  419.8 12.7 %copy-start.94 = (bf16[2048,3072]{0,1:T(8,128)(2,1)S(1)}, bf16[2048,3072]{0,1:T(8,128)(2,1)}, u32[]{:S(2)}) copy-start(bf16[2048,3072]{0,1:T(8,128)(2,1)} %all-gather.9.cloned.1.call-done) | copy-start | bytes 37748740
  485.0 14.9 %collective-permute-start.20 = (bf16[576,2048]{1,0:T(8,128)(2,1)S(1)}, bf16[576,2048]{1,0:T(8,128)(2,1)S(1)}, u32[]{:S(2)}, u32[]{:S(2)}) collective-permute-start(bf16[576,2048]{1,0:T(8,128)(2,1)S(1)} %slice.345), channel_id=1, source_target_pairs={{4,0},{0,4},{5,1},{1,5},{6,2},{2,6},{7,3},{3,7},{12,8},{8,12},{13,... | collective-permute-start | bytes 7077896 | tf_op jit(solution)/shard_map/ppermute | solution.py:161
  499.6 4.6 collective-permute-start.14
  503.1 28.9 %collective-permute-start.21 = (bf16[288,2048]{1,0:T(8,128)(2,1)S(1)}, bf16[288,2048]{1,0:T(8,128)(2,1)S(1)}, u32[]{:S(2)}, u32[]{:S(2)}) collective-permute-start(bf16[288,2048]{1,0:T(8,128)(2,1)S(1)} %slice.349), channel_id=1, source_target_pairs={{1,0},{0,1},{3,2},{2,3},{5,4},{4,5},{7,6},{6,7},{9,8},{8,9},{11,10... | collective-permute-start | bytes 3538952 | tf_op jit(solution)/shard_map/ppermute | solution.py:166
  505.5 51.2 %collective-permute-start.15 = (bf16[288,2048]{1,0:T(8,128)(2,1)S(1)}, bf16[288,2048]{1,0:T(8,128)(2,1)S(1)}, u32[]{:S(2)}, u32[]{:S(2)}) collective-permute-start(bf16[288,2048]{1,0:T(8,128)(2,1)S(1)} %slice.350), channel_id=1, source_target_pairs={{1,0},{0,1},{3,2},{2,3},{5,4},{4,5},{7,6},{6,7},{9,8},{8,9},{11,10... | collective-permute-start | bytes 3538952 | tf_op jit(solution)/shard_map/ppermute | solution.py:166
  561.1 43.2 %copy-start.37 = (bf16[288,2048]{1,0:T(8,128)(2,1)}, bf16[288,2048]{1,0:T(8,128)(2,1)S(1)}, u32[]{:S(2)}) copy-start(bf16[288,2048]{1,0:T(8,128)(2,1)S(1)} %get-tuple-element.482) | copy-start | bytes 3538948
  561.1 27.4 %collective-permute-start.22 = (bf16[288,2048]{1,0:T(8,128)(2,1)S(1)}, bf16[288,2048]{1,0:T(8,128)(2,1)S(1)}, u32[]{:S(2)}, u32[]{:S(2)}) collective-permute-start(bf16[288,2048]{1,0:T(8,128)(2,1)S(1)} %get-tuple-element.482), channel_id=1, source_target_pairs={{1,0},{0,1},{3,2},{2,3},{5,4},{4,5},{7,6},{6,7},{9,8},{8,9},{11,10... | collective-permute-start | bytes 3538952 | tf_op jit(solution)/shard_map/ppermute | solution.py:152
  591.2 13.2 %collective-permute-start.23 = (bf16[576,2048]{1,0:T(8,128)(2,1)}, bf16[576,2048]{1,0:T(8,128)(2,1)}, u32[]{:S(2)}, u32[]{:S(2)}) collective-permute-start(bf16[576,2048]{1,0:T(8,128)(2,1)} %pad_maximum_fusion.9), channel_id=1, source_target_pairs={{4,0},{0,4},{5,1},{1,5},{6,2},{2,6},{7,3},{3,7},{12,8},{8,12},{13,... | collective-permute-start | bytes 7077896 | tf_op jit(solution)/shard_map/ppermute | solution.py:154
  604.3 303.6 %reduce-scatter.4.cloned.1.call-start = ((), (), s32[]{:S(2)}) async-start(), calls=%async_computation.6 | async-start | bytes 7864320 | tf_op jit(solution)/shard_map/reduce_scatter | solution.py:184
  710.9 199.8 %reduce-scatter.6.cloned.1.call-start = ((), (), s32[]{:S(2)}) async-start(), calls=%async_computation.7 | async-start | bytes 15728640 | tf_op jit(solution)/shard_map/reduce_scatter | solution.py:184
  712.5 11.2 %copy-start.97 = (bf16[1152,1536]{1,0:T(8,128)(2,1)S(1)}, bf16[1152,1536]{1,0:T(8,128)(2,1)}, u32[]{:S(2)}) copy-start(bf16[1152,1536]{1,0:T(8,128)(2,1)} %get-tuple-element.496) | copy-start | bytes 10616836
  760.5 4.6 collective-permute-start.24
  760.8 9.6 collective-permute-start.16
  768.4 42.0 %copy-start.9 = (bf16[288,2048]{1,0:T(8,128)(2,1)S(1)}, bf16[288,2048]{1,0:T(8,128)(2,1)}, u32[]{:S(2)}) copy-start(bf16[288,2048]{1,0:T(8,128)(2,1)} %copy-done.7) | copy-start | bytes 3538948
  768.4 42.0 %copy-start.72 = (f32[1,2,8,128]{3,1,2,0:T(2,128)S(1)}, f32[1,2,8,128]{3,1,2,0:T(2,128)}, u32[]{:S(2)}) copy-start(f32[1,2,8,128]{3,1,2,0:T(2,128)} %copy-done.71) | copy-start | bytes 24580
  768.4 42.0 %copy-start.81 = (f32[288]{0:T(512)S(1)}, f32[288]{0:T(512)}, u32[]{:S(2)}) copy-start(f32[288]{0:T(512)} %copy-done.80) | copy-start | bytes 3460
  769.6 40.8 %collective-permute-start.25 = (bf16[288,2048]{1,0:T(8,128)(2,1)}, bf16[288,2048]{1,0:T(8,128)(2,1)S(1)}, u32[]{:S(2)}, u32[]{:S(2)}) collective-permute-start(bf16[288,2048]{1,0:T(8,128)(2,1)} %slice.348), channel_id=1, source_target_pairs={{1,0},{0,1},{3,2},{2,3},{5,4},{4,5},{7,6},{6,7},{9,8},{8,9},{11,10... | collective-permute-start | bytes 3538952 | tf_op jit(solution)/shard_map/ppermute | solution.py:166
  770.4 43.6 %copy-start.78 = (f32[2048]{0:T(1024)S(1)}, f32[2048]{0:T(1024)}, u32[]{:S(2)}) copy-start(f32[2048]{0:T(1024)} %get-tuple-element.424) | copy-start | bytes 24580
  770.4 43.6 %copy-start.88 = (f32[128]{0:T(128)S(1)}, f32[128]{0:T(128)}, u32[]{:S(2)}) copy-start(f32[128]{0:T(128)} %get-tuple-element.430) | copy-start | bytes 1540
  770.4 43.6 %copy-start.89 = (f32[128]{0:T(128)S(1)}, f32[128]{0:T(128)}, u32[]{:S(2)}) copy-start(f32[128]{0:T(128)} %get-tuple-element.428) | copy-start | bytes 1540
  770.4 116.9 %copy-start.83 = (f32[288]{0:T(512)S(1)}, f32[288]{0:T(512)}, u32[]{:S(2)}) copy-start(f32[288]{0:T(512)} %copy-done.82) | copy-start | bytes 3460
  770.4 43.5 %copy-start.43 = (bf16[288,2048]{1,0:T(8,128)(2,1)}, bf16[288,2048]{1,0:T(8,128)(2,1)S(1)}, u32[]{:S(2)}) copy-start(bf16[288,2048]{1,0:T(8,128)(2,1)S(1)} %collective-permute-done.16) | copy-start | bytes 3538948
  893.0 19.9 %collective-permute-start.26 = (bf16[288,2048]{1,0:T(8,128)(2,1)}, bf16[288,2048]{1,0:T(8,128)(2,1)}, u32[]{:S(2)}, u32[]{:S(2)}) collective-permute-start(bf16[288,2048]{1,0:T(8,128)(2,1)} %get-tuple-element.478), channel_id=1, source_target_pairs={{0,0},{2,4},{4,2},{6,6},{1,1},{3,5},{5,3},{7,7},{8,8},{10,12},{12,... | collective-permute-start | bytes 3538952 | tf_op jit(solution)/shard_map/ppermute | solution.py:147
  907.9 8.1 collective-permute-start.31
  910.2 12.9 %collective-permute-start.27 = (bf16[256,1536]{0,1:T(8,128)(2,1)}, bf16[256,1536]{0,1:T(8,128)(2,1)}, u32[]{:S(2)}, u32[]{:S(2)}) collective-permute-start(bf16[256,1536]{0,1:T(8,128)(2,1)} %broadcast_select_fusion.15), channel_id=1, source_target_pairs={{4,0},{0,4},{5,1},{1,5},{6,2},{2,6},{7,3},{3,7},{12,8},{8,12},{13,... | collective-permute-start | bytes 2359304 | tf_op jit(solution)/shard_map/ppermute | solution.py:188
  912.8 12.6 %collective-permute-start.29 = (bf16[256,3072]{0,1:T(8,128)(2,1)S(1)}, bf16[256,3072]{0,1:T(8,128)(2,1)S(1)}, u32[]{:S(2)}, u32[]{:S(2)}) collective-permute-start(bf16[256,3072]{0,1:T(8,128)(2,1)S(1)} %broadcast_select_fusion.3), channel_id=1, source_target_pairs={{4,0},{0,4},{5,1},{1,5},{6,2},{2,6},{7,3},{3,7},{12,8},{8,12},{13,... | collective-permute-start | bytes 4718600 | tf_op jit(solution)/shard_map/ppermute | solution.py:188
  917.0 90.4 %collective-permute-start.32 = (bf16[256,1536]{0,1:T(8,128)(2,1)S(1)}, bf16[256,1536]{0,1:T(8,128)(2,1)S(1)}, u32[]{:S(2)}, u32[]{:S(2)}) collective-permute-start(bf16[256,1536]{0,1:T(8,128)(2,1)S(1)} %broadcast_select_fusion.7), channel_id=1, source_target_pairs={{2,0},{0,2},{3,1},{1,3},{6,4},{4,6},{7,5},{5,7},{10,8},{8,10},{11,... | collective-permute-start | bytes 2359304 | tf_op jit(solution)/shard_map/ppermute | solution.py:190
  925.4 82.0 %copy-start.40 = (bf16[256,1536]{0,1:T(8,128)(2,1)S(1)}, bf16[256,1536]{0,1:T(8,128)(2,1)}, u32[]{:S(2)}) copy-start(bf16[256,1536]{0,1:T(8,128)(2,1)} %copy-done.39) | copy-start | bytes 2359300
  925.4 98.9 %collective-permute-start.28 = (bf16[256,1536]{0,1:T(8,128)(2,1)}, bf16[256,1536]{0,1:T(8,128)(2,1)}, u32[]{:S(2)}, u32[]{:S(2)}) collective-permute-start(bf16[256,1536]{0,1:T(8,128)(2,1)} %broadcast_select_fusion.8), channel_id=1, source_target_pairs={{2,0},{0,2},{3,1},{1,3},{6,4},{4,6},{7,5},{5,7},{10,8},{8,10},{11,... | collective-permute-start | bytes 2359304 | tf_op jit(solution)/shard_map/ppermute | solution.py:190
  927.1 130.9 %collective-permute-start.30 = (bf16[256,3072]{0,1:T(8,128)(2,1)}, bf16[256,3072]{0,1:T(8,128)(2,1)}, u32[]{:S(2)}, u32[]{:S(2)}) collective-permute-start(bf16[256,3072]{0,1:T(8,128)(2,1)} %broadcast_select_fusion), channel_id=1, source_target_pairs={{2,0},{0,2},{3,1},{1,3},{6,4},{4,6},{7,5},{5,7},{10,8},{8,10},{11,... | collective-permute-start | bytes 4718600 | tf_op jit(solution)/shard_map/ppermute | solution.py:190
  (79 other events, 235.3 us)
Sparse Core Ops, SparseCore 0:
  54.3 71.2 all-gather.6
  179.3 123.1 all-gather.8
  333.9 68.6 all-gather.10
  604.4 68.4 reduce-scatter.7
  711.0 68.9 reduce-scatter.3
  783.0 123.3 reduce-scatter.5
